TPU v7x, 32 devices: a whole 2x2x4 slice. The times are simulated.
32 devices in a mesh: rep: 8 (over y, x, core), shard: 4 (over z).
Axes of the slice: x: 2, y: 2, z: 4, core: 2. Of those that a mesh axis runs over, the one named last changes fastest.
Arguments:
- layer_input: bfloat16 [8192, 1024], P(('rep', 'shard')), may hold values from -6 to 6
- query_weight: bfloat16 [1024, 1024], P('shard'), may hold values from -0.1875 to 0.1875
- query_bias: bfloat16 [1024], P('shard'), may hold values from -3 to 3
- key_weight: bfloat16 [1024, 1024], P('shard'), may hold values from -0.1875 to 0.1875
- key_bias: bfloat16 [1024], P('shard'), may hold values from -3 to 3
- value_weight: bfloat16 [1024, 1024], P('shard'), may hold values from -0.1875 to 0.1875
- value_bias: bfloat16 [1024], P('shard'), may hold values from -3 to 3
- output_weight: bfloat16 [1024, 1024], P('shard'), may hold values from -0.75 to 0.75
- output_bias: bfloat16 [1024], P('shard'), may hold values from -2.5 to 2.5
- up_weight: bfloat16 [1024, 4096], P('shard'), may hold values from -0.1875 to 0.1875
- up_bias: bfloat16 [4096], P('shard'), may hold values from -3 to 3
- down_weight: bfloat16 [4096, 1024], P('shard'), may hold values from -0.09375 to 0.09375
- down_bias: bfloat16 [1024], P('shard'), may hold values from -1.1953125 to 1.1953125
- attention_gain_in: bfloat16 [1024], P('shard'), may hold values from 0.25 to 1.75
- attention_gain_out: bfloat16 [1024], P('shard'), may hold values from 0.25 to 1.75
- feedforward_gain_in: bfloat16 [1024], P('shard'), may hold values from 0.25 to 1.75
- feedforward_gain_out: bfloat16 [1024], P('shard'), may hold values from 0.25 to 1.75
- layer_cotangent: bfloat16 [8192, 1024], P(('rep', 'shard')), may hold values from -6 to 6
Outputs:
- layer_output: bfloat16 [8192, 1024], P(('rep', 'shard'))
- input_gradient: float32 [8192, 1024], P(('rep', 'shard'))
- query_weight_gradient: float32 [1024, 1024], P('shard')
- query_bias_gradient: float32 [1024], P('shard')
- key_weight_gradient: float32 [1024, 1024], P('shard')
- key_bias_gradient: float32 [1024], P('shard')
- value_weight_gradient: float32 [1024, 1024], P('shard')
- value_bias_gradient: float32 [1024], P('shard')
- output_weight_gradient: float32 [1024, 1024], P('shard')
- output_bias_gradient: float32 [1024], P('shard')
- up_weight_gradient: float32 [1024, 4096], P('shard')
- up_bias_gradient: float32 [4096], P('shard')
- down_weight_gradient: float32 [4096, 1024], P('shard')
- down_bias_gradient: float32 [1024], P('shard')
- attention_gain_in_gradient: float32 [1024], P('shard')
- attention_gain_out_gradient: float32 [1024], P('shard')
- feedforward_gain_in_gradient: float32 [1024], P('shard')
- feedforward_gain_out_gradient: float32 [1024], P('shard')
All inputs are finite; a program needn't handle non-finite values.
Results may differ from a plain program's by a relative error of at most 0.03.
Values may be sent and summed in bfloat16 or wider, within the bound.
No kernel may reach another device: no remote copies, remote signals or barrier semaphores. Data moves between devices by JAX's collectives and lax.ppermute only.
A program may use at most 256 MiB of HBM per device.

v0:
```python
import functools
import math

import jax
import jax.numpy as jnp
import numpy as np
from jax import lax
from jax.experimental import pallas as pl
from jax.experimental.pallas import tpu as pltpu
from jax.sharding import PartitionSpec as P

HEADS = 16


norm_epsilon = 1e-05


def normalize(values):
    centered = values - jnp.mean(values, axis=-1, keepdims=True)
    inverse = lax.rsqrt(jnp.mean(centered * centered, axis=-1, keepdims=True) + norm_epsilon)
    return (centered * inverse, inverse)


def norm_back(normed, inverse, upstream):
    return inverse * (
        upstream
        - jnp.mean(upstream, axis=-1, keepdims=True)
        - normed * jnp.mean(upstream * normed, axis=-1, keepdims=True)
    )


def rotation(positions, head_dim):
    half_dim = head_dim // 2
    freqs = 10000.0 ** (-jnp.arange(half_dim, dtype=jnp.float32) / half_dim)
    angles = positions.astype(jnp.float32)[:, None] * freqs[None, :]
    return (jnp.cos(angles)[:, None, :], jnp.sin(angles)[:, None, :])


def rotate(tensor, cosines, sines, sign):
    half_dim = tensor.shape[-1] // 2
    first = tensor[..., :half_dim]
    second = tensor[..., half_dim:]
    return jnp.concatenate(
        [first * cosines - sign * second * sines, second * cosines + sign * first * sines], axis=-1
    )


def col_sum(values):
    return jnp.sum(values.astype(jnp.float32), axis=0)


def general_device(
    layer_input,
    query_weight,
    query_bias,
    key_weight,
    key_bias,
    value_weight,
    value_bias,
    output_weight,
    output_bias,
    up_weight,
    up_bias,
    down_weight,
    down_bias,
    attention_gain_in,
    attention_gain_out,
    feedforward_gain_in,
    feedforward_gain_out,
    layer_cotangent,
):
    rows = layer_input.shape[0]
    width = layer_input.shape[1]
    heads = HEADS
    head_dim = width // heads
    seq_rows = rows * lax.axis_size("shard")
    factor = head_dim ** (-0.5)
    positions = lax.axis_index("shard") * rows + jnp.arange(rows, dtype=jnp.int32)
    cosines, sines = rotation(positions, head_dim)
    attention_local = (
        query_weight,
        key_weight,
        value_weight,
        output_weight,
        query_bias,
        key_bias,
        value_bias,
        output_bias,
        attention_gain_in,
        attention_gain_out,
    )
    feed_local = (
        up_weight,
        up_bias,
        down_weight,
        down_bias,
        feedforward_gain_in,
        feedforward_gain_out,
    )
    attention_full = (
        lax.all_gather(attention_local[0], "shard", axis=0, tiled=True),
        lax.all_gather(attention_local[1], "shard", axis=0, tiled=True),
        lax.all_gather(attention_local[2], "shard", axis=0, tiled=True),
        lax.all_gather(attention_local[3], "shard", axis=0, tiled=True),
        lax.all_gather(attention_local[4], "shard", axis=0, tiled=True),
        lax.all_gather(attention_local[5], "shard", axis=0, tiled=True),
        lax.all_gather(attention_local[6], "shard", axis=0, tiled=True),
        lax.all_gather(attention_local[7], "shard", axis=0, tiled=True),
        lax.all_gather(attention_local[8], "shard", axis=0, tiled=True),
        lax.all_gather(attention_local[9], "shard", axis=0, tiled=True),
    )
    (
        query_mat,
        key_mat,
        value_mat,
        out_mat,
        query_shift,
        key_shift,
        value_shift,
        out_shift,
        gain_in_a,
        gain_out_a,
    ) = attention_full
    residual_in = layer_input.astype(jnp.float32)
    normed_a, inverse_a = normalize(residual_in)
    hidden_a = (normed_a * gain_in_a.astype(jnp.float32)).astype(jnp.bfloat16)

    def project(matrix, shift):
        return jnp.dot(hidden_a, matrix, preferred_element_type=jnp.float32) + shift.astype(
            jnp.float32
        )

    query_heads = rotate(
        project(query_mat, query_shift).reshape(rows, heads, head_dim), cosines, sines, 1.0
    ).astype(jnp.bfloat16)
    key_rows = (
        rotate(project(key_mat, key_shift).reshape(rows, heads, head_dim), cosines, sines, 1.0)
        .astype(jnp.bfloat16)
        .reshape(rows, width)
    )
    value_rows = project(value_mat, value_shift).astype(jnp.bfloat16)
    start_state = (
        jnp.full((heads, rows), -1e30, jnp.float32),
        jnp.zeros((heads, rows), jnp.float32),
        jnp.zeros((heads, rows, head_dim), jnp.float32),
    )
    key_piece = lax.all_gather(key_rows, "shard", axis=0, tiled=True)
    value_piece = lax.all_gather(value_rows, "shard", axis=0, tiled=True)
    count = key_piece.shape[0]
    block = math.gcd(count, 512)

    def forward_inner(index, state):
        best, total, accum = state
        offset = index * block
        key_block = lax.dynamic_slice_in_dim(key_piece, offset, block, 0).reshape(
            block, heads, head_dim
        )
        value_block = lax.dynamic_slice_in_dim(value_piece, offset, block, 0).reshape(
            block, heads, head_dim
        )
        key_pos = offset + jnp.arange(block, dtype=jnp.int32)
        allowed = key_pos[None, None, :] <= positions[None, :, None]
        scores = (
            jnp.einsum("qhd,khd->hqk", query_heads, key_block, preferred_element_type=jnp.float32)
            * factor
        )
        scores = jnp.where(allowed, scores, -1e30)
        newest = jnp.maximum(best, jnp.max(scores, axis=-1))
        weights = jnp.where(allowed, jnp.exp(scores - newest[..., None]), 0.0)
        decay = jnp.exp(best - newest)
        total = total * decay + jnp.sum(weights, axis=-1)
        accum = accum * decay[..., None] + jnp.einsum(
            "hqk,khd->hqd",
            weights.astype(jnp.bfloat16),
            value_block,
            preferred_element_type=jnp.float32,
        )
        return (newest, total, accum)

    best, total, accum = lax.fori_loop(0, count // block, forward_inner, start_state)
    logsum = best + jnp.log(total)
    attended = (
        jnp.transpose(accum / total[..., None], (1, 0, 2)).reshape(rows, width).astype(jnp.bfloat16)
    )
    branch_a = jnp.dot(attended, out_mat, preferred_element_type=jnp.float32) + out_shift.astype(
        jnp.float32
    )
    normed_o, inverse_o = normalize(branch_a)
    middle = residual_in + normed_o * gain_out_a.astype(jnp.float32)
    feed_full = (
        lax.all_gather(feed_local[0], "shard", axis=0, tiled=True),
        lax.all_gather(feed_local[1], "shard", axis=0, tiled=True),
        lax.all_gather(feed_local[2], "shard", axis=0, tiled=True),
        lax.all_gather(feed_local[3], "shard", axis=0, tiled=True),
        lax.all_gather(feed_local[4], "shard", axis=0, tiled=True),
        lax.all_gather(feed_local[5], "shard", axis=0, tiled=True),
    )
    up_mat, up_shift, down_mat, down_shift, gain_in_f, gain_out_f = feed_full
    normed_f, inverse_f = normalize(middle)
    hidden_f = (normed_f * gain_in_f.astype(jnp.float32)).astype(jnp.bfloat16)
    pre_act = jnp.dot(hidden_f, up_mat, preferred_element_type=jnp.float32) + up_shift.astype(
        jnp.float32
    )
    activated = jax.nn.gelu(pre_act).astype(jnp.bfloat16)
    branch_f = jnp.dot(activated, down_mat, preferred_element_type=jnp.float32) + down_shift.astype(
        jnp.float32
    )
    normed_d, inverse_d = normalize(branch_f)
    layer_output = (middle + normed_d * gain_out_f.astype(jnp.float32)).astype(jnp.bfloat16)
    feed_back = (
        lax.all_gather(feed_local[0], "shard", axis=0, tiled=True),
        lax.all_gather(feed_local[1], "shard", axis=0, tiled=True),
        lax.all_gather(feed_local[2], "shard", axis=0, tiled=True),
        lax.all_gather(feed_local[3], "shard", axis=0, tiled=True),
        lax.all_gather(feed_local[4], "shard", axis=0, tiled=True),
        lax.all_gather(feed_local[5], "shard", axis=0, tiled=True),
    )
    up_back, up_unused, down_back, down_unused, gain_in_fb, gain_out_fb = feed_back
    upstream = layer_cotangent.astype(jnp.float32)
    grad_gain_out_f = jnp.sum(upstream * normed_d, axis=0)
    d_branch_f = norm_back(normed_d, inverse_d, upstream * gain_out_fb.astype(jnp.float32)).astype(
        jnp.bfloat16
    )
    grad_down = jnp.einsum("tf,td->fd", activated, d_branch_f, preferred_element_type=jnp.float32)
    grad_down_shift = col_sum(d_branch_f)
    d_activated = jnp.einsum("td,fd->tf", d_branch_f, down_back, preferred_element_type=jnp.float32)
    gelu_out, gelu_pull = jax.vjp(jax.nn.gelu, pre_act)
    d_pre = gelu_pull(d_activated)[0].astype(jnp.bfloat16)
    grad_up = jnp.einsum("td,tf->df", hidden_f, d_pre, preferred_element_type=jnp.float32)
    grad_up_shift = col_sum(d_pre)
    d_hidden_f = jnp.einsum("tf,df->td", d_pre, up_back, preferred_element_type=jnp.float32)
    grad_gain_in_f = jnp.sum(d_hidden_f * normed_f, axis=0)
    d_middle = upstream + norm_back(
        normed_f, inverse_f, d_hidden_f * gain_in_fb.astype(jnp.float32)
    )
    feed_grads = (
        lax.psum_scatter(
            grad_up.astype(jnp.bfloat16), "shard", scatter_dimension=0, tiled=True
        ).astype(jnp.float32),
        lax.psum_scatter(
            grad_up_shift.astype(jnp.bfloat16), "shard", scatter_dimension=0, tiled=True
        ).astype(jnp.float32),
        lax.psum_scatter(
            grad_down.astype(jnp.bfloat16), "shard", scatter_dimension=0, tiled=True
        ).astype(jnp.float32),
        lax.psum_scatter(
            grad_down_shift.astype(jnp.bfloat16), "shard", scatter_dimension=0, tiled=True
        ).astype(jnp.float32),
        lax.psum_scatter(
            grad_gain_in_f.astype(jnp.bfloat16), "shard", scatter_dimension=0, tiled=True
        ).astype(jnp.float32),
        lax.psum_scatter(
            grad_gain_out_f.astype(jnp.bfloat16), "shard", scatter_dimension=0, tiled=True
        ).astype(jnp.float32),
    )
    attention_back = (
        lax.all_gather(attention_local[0], "shard", axis=0, tiled=True),
        lax.all_gather(attention_local[1], "shard", axis=0, tiled=True),
        lax.all_gather(attention_local[2], "shard", axis=0, tiled=True),
        lax.all_gather(attention_local[3], "shard", axis=0, tiled=True),
        lax.all_gather(attention_local[4], "shard", axis=0, tiled=True),
        lax.all_gather(attention_local[5], "shard", axis=0, tiled=True),
        lax.all_gather(attention_local[6], "shard", axis=0, tiled=True),
        lax.all_gather(attention_local[7], "shard", axis=0, tiled=True),
        lax.all_gather(attention_local[8], "shard", axis=0, tiled=True),
        lax.all_gather(attention_local[9], "shard", axis=0, tiled=True),
    )
    (
        query_back,
        key_back,
        value_back,
        out_back,
        qshift_unused,
        kshift_unused,
        vshift_unused,
        oshift_unused,
        gain_in_ab,
        gain_out_ab,
    ) = attention_back
    grad_gain_out_a = jnp.sum(d_middle * normed_o, axis=0)
    d_branch_a = norm_back(normed_o, inverse_o, d_middle * gain_out_ab.astype(jnp.float32)).astype(
        jnp.bfloat16
    )
    grad_out_mat = jnp.einsum("td,te->de", attended, d_branch_a, preferred_element_type=jnp.float32)
    grad_out_shift = col_sum(d_branch_a)
    d_attended = jnp.einsum(
        "te,de->td", d_branch_a, out_back, preferred_element_type=jnp.float32
    ).astype(jnp.bfloat16)
    d_heads = d_attended.reshape(rows, heads, head_dim)
    row_delta = jnp.einsum(
        "qhd,qhd->hq",
        d_heads.astype(jnp.float32),
        attended.reshape(rows, heads, head_dim).astype(jnp.float32),
    )

    def query_terms(key_block, value_block, key_pos):
        allowed = key_pos[None, None, :] <= positions[None, :, None]
        scores = (
            jnp.einsum("qhd,khd->hqk", query_heads, key_block, preferred_element_type=jnp.float32)
            * factor
        )
        probs = jnp.where(allowed, jnp.exp(scores - logsum[..., None]), 0.0)
        d_probs = jnp.einsum(
            "qhd,khd->hqk", d_heads, value_block, preferred_element_type=jnp.float32
        )
        d_scores = (probs * (d_probs - row_delta[..., None])).astype(jnp.bfloat16)
        return (probs, d_scores)

    back_state = (
        jnp.zeros((rows, heads, head_dim), jnp.float32),
        jnp.zeros((seq_rows, width), jnp.float32),
        jnp.zeros((seq_rows, width), jnp.float32),
    )
    backward_key_piece = lax.all_gather(key_rows, "shard", axis=0, tiled=True)
    backward_value_piece = lax.all_gather(value_rows, "shard", axis=0, tiled=True)
    count = backward_key_piece.shape[0]
    backward_block = math.gcd(count, 512)

    def backward_inner(index, state):
        grad_query, grad_keys, grad_values = state
        offset = index * backward_block
        key_block = lax.dynamic_slice_in_dim(backward_key_piece, offset, backward_block, 0).reshape(
            backward_block, heads, head_dim
        )
        value_block = lax.dynamic_slice_in_dim(
            backward_value_piece, offset, backward_block, 0
        ).reshape(backward_block, heads, head_dim)
        key_pos = offset + jnp.arange(backward_block, dtype=jnp.int32)
        probs, d_scores = query_terms(key_block, value_block, key_pos)
        grad_query = (
            grad_query
            + jnp.einsum("hqk,khd->qhd", d_scores, key_block, preferred_element_type=jnp.float32)
            * factor
        )
        key_grad = (
            jnp.einsum("hqk,qhd->khd", d_scores, query_heads, preferred_element_type=jnp.float32)
            * factor
        )
        value_grad = jnp.einsum(
            "hqk,qhd->khd", probs.astype(jnp.bfloat16), d_heads, preferred_element_type=jnp.float32
        )
        grad_keys = lax.dynamic_update_slice_in_dim(
            grad_keys, key_grad.reshape(backward_block, width), offset, 0
        )
        grad_values = lax.dynamic_update_slice_in_dim(
            grad_values, value_grad.reshape(backward_block, width), offset, 0
        )
        return (grad_query, grad_keys, grad_values)

    back_result = lax.fori_loop(0, count // backward_block, backward_inner, back_state)
    grad_query = back_result[0]
    key_total, value_total = (
        lax.psum_scatter(
            back_result[1].astype(jnp.bfloat16), "shard", scatter_dimension=0, tiled=True
        ).astype(jnp.float32),
        lax.psum_scatter(
            back_result[2].astype(jnp.bfloat16), "shard", scatter_dimension=0, tiled=True
        ).astype(jnp.float32),
    )
    d_query = rotate(grad_query, cosines, sines, -1.0).reshape(rows, width).astype(jnp.bfloat16)
    d_key = (
        rotate(key_total.reshape(rows, heads, head_dim), cosines, sines, -1.0)
        .reshape(rows, width)
        .astype(jnp.bfloat16)
    )
    d_value = value_total.astype(jnp.bfloat16)
    grad_query_mat = jnp.einsum("td,te->de", hidden_a, d_query, preferred_element_type=jnp.float32)
    grad_key_mat = jnp.einsum("td,te->de", hidden_a, d_key, preferred_element_type=jnp.float32)
    grad_value_mat = jnp.einsum("td,te->de", hidden_a, d_value, preferred_element_type=jnp.float32)
    d_hidden_a = jnp.einsum("te,de->td", d_query, query_back, preferred_element_type=jnp.float32)
    d_hidden_a = d_hidden_a + jnp.einsum(
        "te,de->td", d_key, key_back, preferred_element_type=jnp.float32
    )
    d_hidden_a = d_hidden_a + jnp.einsum(
        "te,de->td", d_value, value_back, preferred_element_type=jnp.float32
    )
    grad_gain_in_a = jnp.sum(d_hidden_a * normed_a, axis=0)
    input_gradient = d_middle + norm_back(
        normed_a, inverse_a, d_hidden_a * gain_in_ab.astype(jnp.float32)
    )
    attention_grads = (
        lax.psum_scatter(
            grad_query_mat.astype(jnp.bfloat16), "shard", scatter_dimension=0, tiled=True
        ).astype(jnp.float32),
        lax.psum_scatter(
            grad_key_mat.astype(jnp.bfloat16), "shard", scatter_dimension=0, tiled=True
        ).astype(jnp.float32),
        lax.psum_scatter(
            grad_value_mat.astype(jnp.bfloat16), "shard", scatter_dimension=0, tiled=True
        ).astype(jnp.float32),
        lax.psum_scatter(
            grad_out_mat.astype(jnp.bfloat16), "shard", scatter_dimension=0, tiled=True
        ).astype(jnp.float32),
        lax.psum_scatter(
            col_sum(d_query).astype(jnp.bfloat16), "shard", scatter_dimension=0, tiled=True
        ).astype(jnp.float32),
        lax.psum_scatter(
            col_sum(d_key).astype(jnp.bfloat16), "shard", scatter_dimension=0, tiled=True
        ).astype(jnp.float32),
        lax.psum_scatter(
            col_sum(d_value).astype(jnp.bfloat16), "shard", scatter_dimension=0, tiled=True
        ).astype(jnp.float32),
        lax.psum_scatter(
            grad_out_shift.astype(jnp.bfloat16), "shard", scatter_dimension=0, tiled=True
        ).astype(jnp.float32),
        lax.psum_scatter(
            grad_gain_in_a.astype(jnp.bfloat16), "shard", scatter_dimension=0, tiled=True
        ).astype(jnp.float32),
        lax.psum_scatter(
            grad_gain_out_a.astype(jnp.bfloat16), "shard", scatter_dimension=0, tiled=True
        ).astype(jnp.float32),
    )
    (
        g_query,
        g_key,
        g_value,
        g_out,
        g_qshift,
        g_kshift,
        g_vshift,
        g_oshift,
        g_gain_in_a,
        g_gain_out_a,
    ) = attention_grads
    g_up, g_up_shift, g_down, g_down_shift, g_gain_in_f, g_gain_out_f = feed_grads
    summed = (
        lax.psum(g_query.astype(jnp.bfloat16), "rep").astype(jnp.float32),
        lax.psum(g_qshift.astype(jnp.bfloat16), "rep").astype(jnp.float32),
        lax.psum(g_key.astype(jnp.bfloat16), "rep").astype(jnp.float32),
        lax.psum(g_kshift.astype(jnp.bfloat16), "rep").astype(jnp.float32),
        lax.psum(g_value.astype(jnp.bfloat16), "rep").astype(jnp.float32),
        lax.psum(g_vshift.astype(jnp.bfloat16), "rep").astype(jnp.float32),
        lax.psum(g_out.astype(jnp.bfloat16), "rep").astype(jnp.float32),
        lax.psum(g_oshift.astype(jnp.bfloat16), "rep").astype(jnp.float32),
        lax.psum(g_up.astype(jnp.bfloat16), "rep").astype(jnp.float32),
        lax.psum(g_up_shift.astype(jnp.bfloat16), "rep").astype(jnp.float32),
        lax.psum(g_down.astype(jnp.bfloat16), "rep").astype(jnp.float32),
        lax.psum(g_down_shift.astype(jnp.bfloat16), "rep").astype(jnp.float32),
        lax.psum(g_gain_in_a.astype(jnp.bfloat16), "rep").astype(jnp.float32),
        lax.psum(g_gain_out_a.astype(jnp.bfloat16), "rep").astype(jnp.float32),
        lax.psum(g_gain_in_f.astype(jnp.bfloat16), "rep").astype(jnp.float32),
        lax.psum(g_gain_out_f.astype(jnp.bfloat16), "rep").astype(jnp.float32),
    )
    return (
        layer_output,
        input_gradient,
        summed[0],
        summed[1],
        summed[2],
        summed[3],
        summed[4],
        summed[5],
        summed[6],
        summed[7],
        summed[8],
        summed[9],
        summed[10],
        summed[11],
        summed[12],
        summed[13],
        summed[14],
        summed[15],
    )


CORE, X, Y = 1, 2, 4
GROUP = 4
BLOCK = 256


def swap(values, bit):
    count = lax.axis_size("rep")
    return lax.ppermute(values, "rep", [(i, i ^ bit) for i in range(count)])


def shift(values, step):
    count = lax.axis_size("shard")
    return lax.ppermute(values, "shard", [(i, (i + step) % count) for i in range(count)])


def flip(values, bit):
    count = lax.axis_size("shard")
    return lax.ppermute(values, "shard", [(i, i ^ bit) for i in range(count)])


def token_pairs(count):
    pairs = []
    for rep in range(count):
        for z in range(GROUP):
            there = (rep & ~3) | ((z & 1) << 1) | (z >> 1)
            pairs.append((rep * GROUP + z, there * GROUP + ((rep >> 1) & 1) + 2 * (rep & 1)))
    return pairs


def spot():
    rep, place = lax.axis_index("rep"), lax.axis_index("shard")
    return rep & 3, place, rep >> 2, ((rep >> 1) & 1) + 2 * (rep & 1)


def aligned(index, size):
    return pl.ds(pl.multiple_of(index * size, size), size)


def dot(left, right):
    return jnp.dot(left, right, preferred_element_type=jnp.float32)


def nt(left, right):
    return lax.dot_general(left, right, (((1,), (1,)), ((), ())), preferred_element_type=jnp.float32)


def tn(left, right):
    return lax.dot_general(left, right, (((0,), (0,)), ((), ())), preferred_element_type=jnp.float32)


def rounded(values):
    return values.astype(jnp.bfloat16)


def wide(values):
    return values.astype(jnp.float32)


def shaped(*dims, kind=jnp.bfloat16):
    return jax.ShapeDtypeStruct(dims, kind)


VMEM_SPEC = pl.BlockSpec(memory_space=pltpu.VMEM)


def call(kernel, outs, *operands, scratch=(), flops=0, exps=0, room=6):
    size = lambda items: sum(math.prod(item.shape) * item.dtype.itemsize for item in items)
    moved = size(operands) + size(outs)
    spaces = [jax.ShapeDtypeStruct(item.shape, item.dtype) for item in scratch]
    return pl.pallas_call(
        kernel,
        out_shape=tuple(outs),
        in_specs=[VMEM_SPEC] * len(operands),
        out_specs=tuple([VMEM_SPEC] * len(outs)),
        scratch_shapes=list(scratch),
        compiler_params=pltpu.CompilerParams(vmem_limit_bytes=moved + size(spaces) + (room << 20)),
        cost_estimate=pl.CostEstimate(flops=flops // 40, bytes_accessed=moved // 40, transcendentals=0),
        name=kernel.__name__,
    )(*operands)


def standardize(values):
    centered = values - jnp.mean(values, axis=-1, keepdims=True)
    inverse = lax.rsqrt(jnp.mean(centered * centered, axis=-1, keepdims=True) + norm_epsilon)
    return centered * inverse, inverse


def turn(values, cosines, sines):
    lane = lax.broadcasted_iota(jnp.int32, values.shape, 1)
    swapped = jnp.where(lane % 64 < 32, pltpu.roll(values, 96, 1), pltpu.roll(values, 32, 1))
    return values * cosines + swapped * sines


def rope_tables(tokens, head_dim):
    half = head_dim // 2
    freqs = 10000.0 ** (-jnp.arange(half, dtype=jnp.float32) / half)
    angles = jnp.arange(tokens, dtype=jnp.int32).astype(jnp.float32)[:, None] * freqs[None, :]
    cosines, sines = jnp.cos(angles), jnp.sin(angles)
    return (
        jnp.concatenate([cosines] * 4, 1),
        jnp.concatenate([-sines, sines, -sines, sines], 1),
    )


def pack_attention(
    query_weight, key_weight, value_weight, out_weight, qb, kb, vb, ub, ob, db, ga, gb, gc, gd, packed
):
    quarter, place, _, _ = spot()
    row = lax.broadcasted_iota(jnp.int32, (1024, 256), 0)
    col = lax.broadcasted_iota(jnp.int32, (1024, 256), 1)
    chosen = rounded(wide(row == (col // 64) * 256 + quarter * 64 + col % 64))
    for index, weight in enumerate((query_weight, key_weight, value_weight)):
        mine = rounded(dot(weight[...], chosen))
        for half in range(2):
            packed[half, :128, index * 256 : index * 256 + 256] = mine[half * 128 : half * 128 + 128]
    out_mine = out_weight[aligned(quarter, 64), :]
    for j in range(4):
        at = (j % 2) * 64
        packed[j // 2, at : at + 64, 768:1024] = out_mine[:, j * 256 : j * 256 + 256]
    row = lax.broadcasted_iota(jnp.int32, (256, 256), 0)
    col = lax.broadcasted_iota(jnp.int32, (256, 256), 1)
    chosen = rounded(wide((row == quarter * 64 + col % 64) & (col // 64 == place)))
    biases = [dot(jnp.broadcast_to(item[...][None, :], (16, 256)), chosen) for item in (qb, kb, vb)]
    full = lambda item: jnp.broadcast_to(wide(item[...])[None, :], (16, 256))
    up_mine = jnp.broadcast_to(wide(ub[aligned(quarter, 256)])[None, :], (16, 256))
    zero = jnp.zeros((16, 256), jnp.float32)
    first = jnp.concatenate(biases + [zero], 1)
    second = jnp.concatenate([up_mine, full(ob), full(db), zero], 1)
    third = jnp.concatenate([full(ga), full(gb), full(gc), full(gd)], 1)
    at = lax.broadcasted_iota(jnp.int32, (16, 1024), 0)
    rows = jnp.where(at == 0, first, jnp.where(at == 1, second, jnp.where(at == 2, third, 0.0)))
    for half in range(2):
        packed[half, 128:144, :] = rounded(rows)


def pack_feed(up_weight, down_weight, up_packed, down_packed, sems):
    quarter, _, _, _ = spot()
    copies = []
    for half in range(2):
        for there in range(4):
            lanes = pl.ds(pl.multiple_of(there * 1024 + quarter * 256, 256), 256)
            copies.append(
                (
                    up_weight.at[half * 128 : half * 128 + 128, lanes],
                    up_packed.at[half, :, there * 256 : there * 256 + 256],
                )
            )
        copies.append((down_weight.at[aligned(quarter * 2 + half, 128), :], down_packed.at[half]))
    copies = [pltpu.make_async_copy(a, b, sems.at[i]) for i, (a, b) in enumerate(copies)]
    for copy in copies:
        copy.start()
    for copy in copies:
        copy.wait()


def call_pack_feed(up_weight, down_weight):
    spec = pl.BlockSpec(memory_space=pl.ANY)
    return pl.pallas_call(
        pack_feed,
        out_shape=(shaped(2, 128, 1024), shaped(2, 128, 1024)),
        in_specs=[spec, spec],
        out_specs=(VMEM_SPEC, VMEM_SPEC),
        scratch_shapes=[pltpu.SemaphoreType.DMA((10,))],
        compiler_params=pltpu.CompilerParams(vmem_limit_bytes=8 << 20),
        cost_estimate=pl.CostEstimate(flops=0, bytes_accessed=2 << 20, transcendentals=0),
        name="pack_feed",
    )(up_weight, down_weight)


def tie(value, *earlier):
    return lax.optimization_barrier((value, *earlier))[0]


def near_pieces(packed, half, *earlier, direct=False):
    mine = tie(lax.dynamic_index_in_dim(packed, half, 0, False), *earlier)
    if direct:
        return [flip(mine, step) for step in (1, 2, 3)]
    second = flip(mine, 2)
    return [flip(mine, 1), second, flip(second, 1)]


def far_pieces(near):
    return [swap(item, Y) for item in near]


def far_together(near):
    return swap(jnp.stack(near), Y)


def each_piece(own, near, far):
    _, place, y_bit, _ = spot()
    yield place, 0, own.at[0]
    yield place, 1, own.at[1]
    for step in (1, 2, 3):
        yield place ^ step, y_bit, near[step - 1]
        yield place ^ step, 1 - y_bit, far[step - 1]


def head_lanes(shape, parity):
    return (lax.broadcasted_iota(jnp.int32, shape, 1) // 64) == parity


def causal_block():
    shape = (BLOCK, BLOCK)
    return lax.broadcasted_iota(jnp.int32, shape, 0) >= lax.broadcasted_iota(jnp.int32, shape, 1)


def attend(
    x0, x1, x2, x3, own, z1, z2, z3, y1, y2, y3, cosines, sines,
    query, key, value, mixed, logs, hidden, qkv, out_rows, vectors, p0, p1, p32,
):
    _, _, _, position = spot()
    for relative, rows_in in enumerate((x0, x1, x2, x3)):
        hidden[aligned(position ^ relative, BLOCK), :] = rows_in[...]
    vectors[...] = jnp.zeros_like(vectors)
    for index, (shard, half, piece) in enumerate(each_piece(own, (z1, z2, z3), (y1, y2, y3))):
        qkv[aligned(shard * 2 + half, 128), :] = piece[:128, :768]
        for j in range(2):
            out_rows[aligned(shard, 64), aligned(half * 2 + j, 256)] = piece[j * 64 : j * 64 + 64, 768:]
        if index == 0 or index >= 2 and index % 2 == 0:
            small = wide(piece[128:144, :])
            lanes = aligned(shard, 256)
            vectors[0:1, lanes] = small[1:2, 256:512]
            vectors[1:2, lanes] = small[1:2, 512:768]
            for gain in range(4):
                vectors[2 + gain : 3 + gain, lanes] = small[2:3, gain * 256 : gain * 256 + 256]
            vectors[6:7, lanes] = small[1:2, :256]
            vectors[7:8, :] += small[0:1, :]

    def project(index, carry):
        rows = aligned(index, BLOCK)
        normed, _ = standardize(wide(hidden[rows, :]))
        block = rounded(normed * vectors[2:3, :])
        hidden[rows, :] = block
        raw = dot(block, qkv[...]) + vectors[7:8, :768]
        cos, sin = cosines[rows, :], sines[rows, :]
        for tile in range(2):
            at = tile * 128
            lanes = slice(at, at + 128)
            query[rows, lanes] = rounded(turn(raw[:, lanes], cos, sin)) * jnp.bfloat16(0.125)
            key[rows, lanes] = rounded(turn(raw[:, 256 + at : 384 + at], cos, sin))
        value[rows, :] = rounded(raw[:, 512:])
        return carry

    lax.fori_loop(0, GROUP, project, 0)
    causal = causal_block()
    logs[...] = jnp.zeros_like(logs)
    mixed[...] = jnp.zeros_like(mixed)
    lane = lax.broadcasted_iota(jnp.int32, (BLOCK, 128), 1)

    def head(index, carry):
        lanes = aligned(index >> 1, 128)
        mine = lane // 64 == (index & 1)
        for block in range(GROUP):
            rows = slice(block * BLOCK, block * BLOCK + BLOCK)
            seen = (block + 1) * BLOCK
            masked = jnp.where(mine, query[rows, lanes], jnp.bfloat16(0))
            scores = nt(masked, key[:seen, lanes])
            last = jnp.where(causal, scores[:, seen - BLOCK :], -1e30)
            scores = jnp.concatenate([scores[:, : seen - BLOCK], last], 1) if block else last
            best = jnp.max(scores, axis=1, keepdims=True)
            exps = jnp.exp(scores - best)
            total = jnp.sum(exps, axis=1, keepdims=True)
            out = dot(rounded(exps), value[:seen, lanes]) / total
            mixed[rows, lanes] = jnp.where(mine, rounded(out), mixed[rows, lanes])
            logs[rows, :] = jnp.where(lane == index, best + jnp.log(total), logs[rows, :])
        return carry

    lax.fori_loop(0, 4, head, 0)
    for relative, part in enumerate((p0, p1, p32.at[BLOCK:], p32.at[:BLOCK])):
        part[...] = rounded(dot(mixed[aligned(position ^ relative, BLOCK), :], out_rows[...]))


def pair_back(pair, query, key, value, mixed, logs, d_out, d_query, d_key, d_value):
    lanes = slice(pair * 128, pair * 128 + 128)
    causal = causal_block()
    lane = lax.broadcasted_iota(jnp.int32, (BLOCK, 128), 1)
    d_key[...] = jnp.zeros_like(d_key)
    d_value[...] = jnp.zeros_like(d_value)
    d_query[...] = jnp.zeros_like(d_query)

    def head(parity, carry):
        mine = lane // 64 == parity
        for block in range(GROUP):
            rows = slice(block * BLOCK, block * BLOCK + BLOCK)
            seen = (block + 1) * BLOCK
            keys, values = key[:seen, lanes], value[:seen, lanes]
            masked_q = jnp.where(mine, query[rows, lanes], jnp.bfloat16(0))
            masked_d = jnp.where(mine, d_out[rows, lanes], jnp.bfloat16(0))
            log = jnp.sum(jnp.where(lane == pair * 2 + parity, logs[rows, :], 0.0), 1, keepdims=True)
            delta = jnp.sum(wide(masked_d) * wide(mixed[rows, lanes]), 1, keepdims=True)
            probs = jnp.exp(nt(masked_q, keys) - log)
            last = jnp.where(causal, probs[:, seen - BLOCK :], 0.0)
            probs = jnp.concatenate([probs[:, : seen - BLOCK], last], 1) if block else last
            d_scores = rounded(probs * (nt(masked_d, values) - delta))
            d_query[rows, :] += jnp.where(mine, dot(d_scores, keys), 0.0)
            d_value[:seen, :] += tn(rounded(probs), masked_d)
            d_key[:seen, :] += tn(d_scores, masked_q)
        return carry

    lax.fori_loop(0, 2, head, 0)


def finish_back(cosines, sines, d_query, d_key, d_value, grads, shift_sums):
    shift_sums[...] = jnp.zeros_like(shift_sums)

    def finish(index, carry):
        rows = aligned(index, BLOCK)
        cos, sin = cosines[rows, :], -sines[rows, :]
        grads[rows, :128] = rounded(turn(d_query[rows, :] * 0.125, cos, sin))
        grads[rows, 128:256] = rounded(turn(d_key[rows, :], cos, sin))
        grads[rows, 256:] = rounded(d_value[rows, :])
        shift_sums[0:1, :] += jnp.sum(wide(grads[rows, :]), axis=0, keepdims=True)
        return carry

    lax.fori_loop(0, GROUP, finish, 0)


def attend_back_first(
    a0, a1, a2, a3, out_rows, query, key, value, mixed, logs, cosines, sines,
    d_out, grads, shift_sums, d_query, d_key, d_value,
):
    _, _, _, position = spot()
    for relative, rows_in in enumerate((a0, a1, a2, a3)):
        d_out[aligned(position ^ relative, BLOCK), :] = rounded(nt(rows_in[...], out_rows[...]))
    pair_back(0, query, key, value, mixed, logs, d_out, d_query, d_key, d_value)
    finish_back(cosines, sines, d_query, d_key, d_value, grads, shift_sums)


def attend_back_second(
    d_out, before, qkv, query, key, value, mixed, logs, cosines, sines,
    grads, shift_sums, p0, p1, p32, d_query, d_key, d_value, joined,
):
    _, _, _, position = spot()
    pair_back(1, query, key, value, mixed, logs, d_out, d_query, d_key, d_value)
    finish_back(cosines, sines, d_query, d_key, d_value, grads, shift_sums)
    for index in range(3):
        joined[:, index * 256 : index * 256 + 128] = before[:, index * 128 : index * 128 + 128]
        joined[:, index * 256 + 128 : index * 256 + 256] = grads[:, index * 128 : index * 128 + 128]
    for relative, part in enumerate((p0, p1, p32.at[BLOCK:], p32.at[:BLOCK])):
        part[...] = rounded(nt(joined[aligned(position ^ relative, BLOCK), :], qkv[...]))


CHUNK = 64


def in_chunks(step):
    def one(index, carry):
        step(aligned(index, CHUNK), pl.ds(pl.multiple_of(BLOCK + index * CHUNK, CHUNK), CHUNK))
        return carry

    lax.fori_loop(0, BLOCK // CHUNK, one, 0)


def after_attention(p0, core_in, x_in, rows_in, vectors, middle, hidden, normed_o, normed_f, inverses):
    def step(rows, low):
        branch = wide(p0[rows, :]) + wide(core_in[low, :]) + wide(x_in[rows, :]) + vectors[0:1, :]
        normed, inverse_o = standardize(branch)
        normed_o[rows, :] = normed
        total = wide(rows_in[rows, :]) + normed * vectors[3:4, :]
        middle[rows, :] = total
        normed, inverse_f = standardize(total)
        normed_f[rows, :] = normed
        hidden[rows, :] = rounded(normed * vectors[4:5, :])
        lane = lax.broadcasted_iota(jnp.int32, (CHUNK, 128), 1)
        inverses[rows, :] = jnp.where(lane < 64, inverse_o, inverse_f)

    in_chunks(step)


def after_feed(p0, core_in, x_in, middle, cotangent, vectors, layer_out, d_branch, sums):
    sums[...] = jnp.zeros_like(sums)

    def step(rows, low):
        branch = wide(p0[rows, :]) + wide(core_in[low, :]) + wide(x_in[rows, :]) + vectors[1:2, :]
        normed, inverse = standardize(branch)
        gain = vectors[5:6, :]
        layer_out[rows, :] = rounded(middle[rows, :] + normed * gain)
        upstream = wide(cotangent[rows, :])
        back = rounded(norm_back(normed, inverse, upstream * gain))
        d_branch[rows, :] = back
        sums[0:1, :] += jnp.sum(upstream * normed, axis=0, keepdims=True)
        sums[1:2, :] += jnp.sum(wide(back), axis=0, keepdims=True)

    in_chunks(step)


def after_feed_back(
    p0, core_in, x_in, cotangent, normed_o, normed_f, inverses, vectors, d_middle, d_branch, sums
):
    sums[...] = jnp.zeros_like(sums)

    def step(rows, low):
        d_hidden = wide(p0[rows, :]) + wide(core_in[low, :]) + wide(x_in[rows, :])
        normed = normed_f[rows, :]
        sums[0:1, :] += jnp.sum(d_hidden * normed, axis=0, keepdims=True)
        total = wide(cotangent[rows, :]) + norm_back(
            normed, inverses[rows, 64:65], d_hidden * vectors[4:5, :]
        )
        d_middle[rows, :] = total
        normed = normed_o[rows, :]
        sums[1:2, :] += jnp.sum(total * normed, axis=0, keepdims=True)
        back = rounded(norm_back(normed, inverses[rows, 0:1], total * vectors[3:4, :]))
        d_branch[rows, :] = back
        sums[2:3, :] += jnp.sum(wide(back), axis=0, keepdims=True)

    in_chunks(step)


def gain_in_sums(p0, p1, p32, x0, x1, x2, x3, sums):
    sums[...] = jnp.zeros_like(sums)

    def step(rows, low):
        for part, rows_in in ((p0[rows, :], x0), (p1[rows, :], x1), (p32[low, :], x2), (p32[rows, :], x3)):
            normed, _ = standardize(wide(rows_in[rows, :]))
            sums[0:1, :] += jnp.sum(wide(part) * normed, axis=0, keepdims=True)

    in_chunks(step)


def after_attention_back(p0, core_in, x_in, rows_in, d_middle, vectors, d_rows):
    def step(rows, low):
        d_hidden = wide(p0[rows, :]) + wide(core_in[low, :]) + wide(x_in[rows, :])
        normed, inverse = standardize(wide(rows_in[rows, :]))
        d_rows[rows, :] = rounded(
            d_middle[rows, :] + norm_back(normed, inverse, d_hidden * vectors[2:3, :])
        )

    in_chunks(step)


GELU_SCALE = math.sqrt(2.0 / math.pi)


def feed_rows(rows_in, up_mat, down_mat, vectors, before, after, part, at):
    rows = slice(at, at + BLOCK)

    def step(index, carry):
        lanes = aligned(index, BLOCK)
        raw = dot(rows_in[...], up_mat[:, lanes]) + vectors[6:7, lanes]
        before[rows, lanes] = raw
        after[rows, lanes] = rounded(jax.nn.gelu(raw))
        return carry

    lax.fori_loop(0, 4, step, 0)

    def out(index, carry):
        lanes = aligned(index, BLOCK)
        part[:, lanes] = rounded(dot(after[rows, :], down_mat[:, lanes]))
        return carry

    lax.fori_loop(0, 4, out, 0)


def feed_first(
    h0, h2, uo, u1, u2, u3, far_u, do, d1, d2, d3, far_d, vectors,
    up_mat, down_mat, before, after, p0, p2,
):
    for shard, half, piece in each_piece(uo, (u1, u2, u3), [far_u.at[i] for i in range(3)]):
        up_mat[aligned(shard * 2 + half, 128), :] = piece[...]
    for shard, half, piece in each_piece(do, (d1, d2, d3), [far_d.at[i] for i in range(3)]):
        down_mat[aligned(shard * 2 + half, 128), :] = piece[...]
    feed_rows(h0, up_mat, down_mat, vectors, before, after, p0, 0)
    feed_rows(h2, up_mat, down_mat, vectors, before, after, p2, BLOCK)


def feed_second(h1, h3, p2, up_mat, down_mat, vectors, before, after, p1, p32):
    p32[BLOCK:, :] = p2[...]
    feed_rows(h3, up_mat, down_mat, vectors, before, after, p32.at[:BLOCK], BLOCK)
    feed_rows(h1, up_mat, down_mat, vectors, before, after, p1, 0)


def feed_back_rows(rows_in, up_mat, down_mat, before, d_pre, part, sums, at):
    rows = slice(at, at + BLOCK)

    def step(index, carry):
        lanes = aligned(index, BLOCK)
        upstream = nt(rows_in[...], down_mat[lanes, :])
        raw = before[rows, lanes]
        square = raw * raw
        bent = jnp.tanh(GELU_SCALE * raw * (1.0 + 0.044715 * square))
        slope = 0.5 * (1.0 + bent) + 0.5 * GELU_SCALE * raw * (1.0 - bent * bent) * (
            1.0 + 3.0 * 0.044715 * square
        )
        back = rounded(upstream * slope)
        d_pre[rows, lanes] = back
        sums[0:1, lanes] += jnp.sum(wide(back), axis=0, keepdims=True)
        return carry

    lax.fori_loop(0, 4, step, 0)

    def out(index, carry):
        lanes = aligned(index, BLOCK)
        part[:, lanes] = rounded(nt(d_pre[rows, :], up_mat[lanes, :]))
        return carry

    lax.fori_loop(0, 4, out, 0)


def feed_back_first(m0, m2, up_mat, down_mat, before, d_pre, p0, p2, sums):
    sums[...] = jnp.zeros_like(sums)
    feed_back_rows(m0, up_mat, down_mat, before, d_pre, p0, sums, 0)
    feed_back_rows(m2, up_mat, down_mat, before, d_pre, p2, sums, BLOCK)


def feed_back_second(m1, m3, p2, up_mat, down_mat, before, sums_in, d_pre, p1, p32, sums):
    sums[...] = sums_in[...]
    p32[BLOCK:, :] = p2[...]
    feed_back_rows(m3, up_mat, down_mat, before, d_pre, p32.at[:BLOCK], sums, BLOCK)
    feed_back_rows(m1, up_mat, down_mat, before, d_pre, p1, sums, 0)


def put_halves(keep, send, step, at, top, bottom):
    _, _, y_bit, _ = spot()

    @pl.when(y_bit == 0)
    def _():
        keep[step, at : at + 128, :] = top
        send[step, at : at + 128, :] = bottom

    @pl.when(y_bit == 1)
    def _():
        keep[step, at : at + 128, :] = bottom
        send[step, at : at + 128, :] = top


def down_grads(first, second, m0, m1, m2, m3, keep, send):
    _, place, _, _ = spot()

    def one(step, carry):
        lanes = aligned(place ^ step, BLOCK)
        down = (
            tn(first[:BLOCK, lanes], m0[...])
            + tn(first[BLOCK:, lanes], m2[...])
            + tn(second[:BLOCK, lanes], m1[...])
            + tn(second[BLOCK:, lanes], m3[...])
        )
        down = rounded(down)
        put_halves(keep, send, step, 0, down[:128], down[128:])
        return carry

    lax.fori_loop(0, 4, one, 0)


def up_grads(h0, h1, h2, h3, u_first, u_second, keep, send):
    _, place, _, _ = spot()

    def one(step, carry):
        lanes = aligned(place ^ step, BLOCK)
        up = (
            tn(h0[:, lanes], u_first[:BLOCK, :])
            + tn(h2[:, lanes], u_first[BLOCK:, :])
            + tn(h1[:, lanes], u_second[:BLOCK, :])
            + tn(h3[:, lanes], u_second[BLOCK:, :])
        )
        up = rounded(up)
        put_halves(keep, send, step, 0, up[:128], up[128:])
        return carry

    lax.fori_loop(0, 4, one, 0)


def attention_grads_first(mixed, a0, a1, a2, a3, hidden, grads, keep, send, out_grad, block):
    _, place, _, position = spot()
    total = tn(mixed[aligned(position, BLOCK), :], a0[...])
    for relative, rows_in in ((1, a1), (2, a2), (3, a3)):
        total = total + tn(mixed[aligned(position ^ relative, BLOCK), :], rows_in[...])
    out_grad[...] = rounded(total)

    def one(step, carry):
        shard = place ^ step
        block[:, :384] = rounded(tn(hidden[:, aligned(shard, BLOCK)], grads[...]))
        mine = out_grad[aligned(shard, 64), :]
        for j in range(4):
            block[j * 64 : j * 64 + 64, 384:] = mine[:, j * 256 : j * 256 + 256]
        put_halves(keep, send, step, 0, block[:128, :], block[128:, :])
        return carry

    lax.fori_loop(0, 4, one, 0)


def attention_grads_second(
    hidden, grads, sums_f, sums_b, sums_a, sums_u, sums_q, sums_r, keep, send
):
    _, place, y_bit, _ = spot()

    def one(step, carry):
        shard = place ^ step
        block = rounded(tn(hidden[:, aligned(shard, BLOCK)], grads[...]))
        put_halves(keep, send, step, 0, block[:128], block[128:])
        lanes = aligned(shard, BLOCK)
        biases = []
        for index in range(3):
            at = index * 128
            pair = jnp.where(shard < 2, sums_q[0:1, at : at + 128], sums_r[0:1, at : at + 128])
            biases.append(jnp.where((shard & 1) == 0, pair[:, :64], pair[:, 64:]))
        zero = jnp.zeros((1, 192), jnp.float32)
        tops = [sums_b[2:3, lanes], sums_f[1:2, lanes], sums_a[0:1, lanes], *biases, zero]
        lows = [sums_b[1:2, lanes], sums_b[0:1, lanes], sums_f[0:1, lanes], sums_u[0:1, lanes], zero[:, :128]]
        halves = []
        for items in (tops, lows):
            flat = jnp.concatenate(items, 1)
            row = lax.broadcasted_iota(jnp.int32, (8, 384), 0)
            full = [jnp.broadcast_to(flat[:, i * 384 : i * 384 + 384], (8, 384)) for i in range(3)]
            rows = jnp.where(row == 0, full[0], jnp.where(row == 1, full[1], full[2]))
            halves.append(rounded(jnp.where(row < 3, rows, 0.0)))
        mine, other = jnp.where(y_bit == 0, halves[0], halves[1]), jnp.where(y_bit == 0, halves[1], halves[0])
        keep[step, 128:136, :] = mine
        send[step, 128:136, :] = other
        return carry

    lax.fori_loop(0, 4, one, 0)


def add_pairs(keep, come, stay, go):
    for step, out in enumerate((stay.at[0], go.at[0], stay.at[1], go.at[1])):
        out[...] = rounded(wide(keep[step]) + wide(come[step]))


def add_near(stay, come, own, go):
    own[...] = rounded(wide(stay[0]) + wide(come[0]))
    go[...] = rounded(wide(stay[1]) + wide(come[1]))


def each_part(own, x_part, y_part, core_part):
    rep = lax.axis_index("rep")
    refs = [own, x_part, y_part.at[0], y_part.at[1]] + [core_part.at[i] for i in range(4)]
    for relative, ref in enumerate(refs):
        flip = ((relative & 1) << 1) | ((relative & 2) << 1) | (relative >> 2)
        there = rep ^ flip
        yield there >> 2, there & 3, ref


def unpack_down(own, x_part, y_part, core_part, down):
    for y_bit, quarter, ref in each_part(own, x_part, y_part, core_part):
        down[aligned(quarter * 2 + y_bit, 128), :] = wide(ref[...])


def unpack_up(own, x_part, y_part, core_part, up):
    for y_bit, quarter, ref in each_part(own, x_part, y_part, core_part):
        for there in range(4):
            lanes = pl.ds(pl.multiple_of(there * 1024 + quarter * 256, 256), 256)
            up[aligned(y_bit, 128), lanes] = wide(ref[:, there * 256 : there * 256 + 256])


def unpack_attention(
    own, x_part, y_part, core_part, own2, x_part2, y_part2, core_part2,
    query, key, value, out_weight, qb, kb, vb, ob, db, ga, gb, gc, gd, ub,
):
    first = list(each_part(own, x_part, y_part, core_part))
    second = list(each_part(own2, x_part2, y_part2, core_part2))
    row = lax.broadcasted_iota(jnp.int32, (128, 512), 0)
    col = lax.broadcasted_iota(jnp.int32, (128, 512), 1)
    sets = ((0, 1, 4, 5), (2, 3, 6, 7))
    chosen = []
    for index in sets[0]:
        quarter = first[index][1]
        chosen.append(rounded(wide(col == (row // 64) * 256 + quarter * 64 + row % 64)))
    chosen = jnp.concatenate(chosen, 0)
    for pair, parts in enumerate((first, second)):
        for members in sets:
            rows = aligned(parts[members[0]][0], 128)
            for index, out in enumerate((query, key, value)):
                lanes = slice(index * 128, index * 128 + 128)
                joined = jnp.concatenate([parts[i][2][:128, lanes] for i in members], 1)
                out[rows, pair * 512 : pair * 512 + 512] = dot(joined, chosen)
    for y_bit, quarter, ref in first:
        for j in range(2):
            out_weight[aligned(quarter, 64), aligned(y_bit * 2 + j, 256)] = wide(
                ref[j * 64 : j * 64 + 64, 384:]
            )
    y_bit = first[0][0]
    flats = []
    for members in sets:
        rows = [wide(second[i][2][128:136, :]) for i in members]
        total = rows[0] + rows[1] + rows[2] + rows[3]
        flats.append((total, rows))
    mine, other = flats
    for half, (outs, size) in enumerate((((ob, db, ga), 64), ((gb, gc, gd), 256))):
        take = y_bit == half
        total = jnp.where(take, mine[0], other[0])
        flat = jnp.concatenate([total[0:1, :], total[1:2, :]], 1)
        for index, out in enumerate(outs):
            out[...] = flat[:, index * 256 : index * 256 + 256]
        locals_ = [jnp.where(take, a, b)[2:3, :] for a, b in zip(mine[1], other[1], strict=True)]
        quarters = [first[i][1] for i in sets[0]]
        for there in range(4):
            value_at = jnp.zeros((1, 384), jnp.float32)
            for quarter, item in zip(quarters, locals_, strict=True):
                value_at = value_at + jnp.where(quarter == there, item, 0.0)
            if half == 0:
                for index, out in enumerate((qb, kb, vb)):
                    out[:, there * 64 : there * 64 + 64] = value_at[:, index * 64 : index * 64 + 64]
            else:
                ub[:, there * 256 : there * 256 + 256] = value_at[:, :256]


def sum_pairs(keep, come):
    two = shaped(2, *keep.shape[1:])
    return call(add_pairs, [two, two], keep, come)


def sum_near(stay, come):
    one = shaped(*stay.shape[1:])
    return call(add_near, [one, one], stay, come)


def sum_far(own, come):
    return rounded(wide(own) + wide(come))


def gather_packs(total):
    x_part = swap(total, X)
    two = jnp.stack([total, x_part])
    y_part = swap(two, Y)
    return total, x_part, y_part, swap(jnp.concatenate([two, y_part]), CORE)


def fast_device(
    layer_input,
    query_weight,
    query_bias,
    key_weight,
    key_bias,
    value_weight,
    value_bias,
    output_weight,
    output_bias,
    up_weight,
    up_bias,
    down_weight,
    down_bias,
    attention_gain_in,
    attention_gain_out,
    feedforward_gain_in,
    feedforward_gain_out,
    layer_cotangent,
):
    f32, bf16 = jnp.float32, jnp.bfloat16
    replicas = lax.axis_size("rep")
    rows, width = layer_input.shape
    tokens = rows * GROUP
    quarter, place, y_bit, _ = spot()
    pairs = token_pairs(replicas)
    back_pairs = [(there, here) for here, there in pairs]
    both = ("rep", "shard")
    part = shaped(rows, width)
    part32 = shaped(rows, width, kind=f32)
    sums = shaped(8, width, kind=f32)

    def spread(piece):
        return swap(piece, X), swap(piece, CORE)

    def gather_sum(p1, p32):
        core_in = swap(p32, CORE)
        return core_in, swap(rounded(wide(p1) + wide(core_in[:rows])), X)

    own_rows = lax.ppermute(layer_input, both, pairs)
    (packed,) = call(
        pack_attention,
        [shaped(2, 144, width)],
        query_weight,
        key_weight,
        value_weight,
        output_weight,
        query_bias,
        key_bias,
        value_bias,
        up_bias,
        output_bias,
        down_bias,
        attention_gain_in,
        attention_gain_out,
        feedforward_gain_in,
        feedforward_gain_out,
    )
    near_a = near_pieces(packed, y_bit)
    cosines, sines = rope_tables(tokens, 64)
    up_packed, down_packed = call_pack_feed(up_weight, down_weight)
    own_rows = tie(own_rows, packed, cosines, sines, up_packed)
    x1, x2 = spread(own_rows)
    blocks = own_rows, x1, x2, swap(x1, CORE)
    far_a = far_pieces(near_a)
    near_u = near_pieces(up_packed, y_bit, *near_a)
    two16 = shaped(2 * rows, width)
    head_rows = shaped(tokens, 256)
    query, key, value, mixed, logs, hidden_a, qkv, out_rows, vectors, p0, p1, p32 = call(
        attend,
        [head_rows] * 4
        + [
            shaped(tokens, 128, kind=f32),
            shaped(tokens, width),
            shaped(width, 768),
            shaped(256, width),
            sums,
        ]
        + [part, part, two16],
        *blocks,
        packed,
        *near_a,
        *far_a,
        cosines,
        sines,
        flops=2 * tokens * 1024 * 1024 + 8 * tokens * tokens * 64 * 2,
        exps=2 * tokens * tokens,
        room=14,
    )
    p32 = tie(p32, *near_u)
    far_u = far_together(near_u)
    near_d = near_pieces(down_packed, y_bit, *near_u)
    core_in, x_in = gather_sum(p1, p32)
    x_in = tie(x_in, far_u, *near_d)
    far_d = far_together(near_d)
    cotangent = lax.ppermute(tie(layer_cotangent, *near_d), both, pairs)
    middle, hidden_own, normed_o, normed_f, inverses = call(
        after_attention,
        [part32, part, part32, part32, shaped(rows, 128, kind=f32)],
        p0,
        core_in,
        x_in,
        own_rows,
        vectors,
    )
    h0 = hidden_own
    h1, h2 = spread(h0)
    two32 = shaped(2 * rows, width, kind=f32)
    square = shaped(width, width)
    flops = 4 * 2 * rows * 1024 * 1024
    up_mat, down_mat, before_a, after_a, p0, p2 = call(
        feed_first,
        [square, square, two32, two16, part, part],
        h0, h2, up_packed, *near_u, far_u, down_packed, *near_d, far_d, vectors,
        flops=flops, room=10,
    )
    h1 = tie(h1, p2, cotangent)
    h3 = swap(h1, CORE)
    before_b, after_b, p1, p32 = call(
        feed_second,
        [two32, two16, part, two16],
        h1, h3, p2, up_mat, down_mat, vectors,
        flops=flops, room=10,
    )
    core_in, x_in = gather_sum(p1, p32)
    layer_output, d_branch, sums_f = call(
        after_feed, [part, part, sums], p0, core_in, x_in, middle, cotangent, vectors
    )
    m0 = d_branch
    m1, m2 = spread(m0)
    u_first, p0, p2, sums_u = call(
        feed_back_first,
        [two16, part, part, sums],
        m0, m2, up_mat, down_mat, before_a,
        flops=flops, room=10,
    )
    m1 = tie(m1, u_first)
    m3 = swap(m1, CORE)
    packs = [shaped(4, 128, width)] * 2
    grad_flops = 2 * tokens * 1024 * 1024
    u_second, p1, p32, sums_u = call(
        feed_back_second,
        [two16, part, two16, sums],
        m1, m3, p2, up_mat, down_mat, before_b, sums_u,
        flops=flops, room=10,
    )
    core_in, x_in = gather_sum(p1, p32)
    pack_d = call(
        down_grads, packs, after_a, after_b, m0, m1, m2, tie(m3, u_second), flops=grad_flops, room=10
    )
    come_d = swap(pack_d[1], Y)
    pack_u = call(
        up_grads,
        packs,
        h0, h1, h2, h3, u_first, tie(u_second, *pack_d),
        flops=grad_flops, room=10,
    )
    flops = grad_flops
    x_in = tie(x_in, *pack_u)
    d_middle, d_branch, sums_b = call(
        after_feed_back,
        [part32, part, sums],
        p0,
        core_in,
        x_in,
        cotangent,
        normed_o,
        normed_f,
        inverses,
        vectors,
    )
    a0 = d_branch
    a1, a2 = spread(a0)
    stay_d, go_d = sum_pairs(tie(pack_d[0], d_branch), come_d)
    come_u = swap(pack_u[1], Y)
    a1 = tie(a1, go_d)
    layer_output = lax.ppermute(tie(layer_output, a1), both, back_pairs)
    a3 = swap(a1, CORE)
    a_blocks = a0, a1, a2, a3
    come_d = flip(go_d, 1)
    grad32 = [pltpu.VMEM((tokens, 128), f32)] * 3
    back_flops = tokens * 1024 * 1024 + 10 * tokens * tokens * 64 * 2
    d_out, grads_first, sums_q = call(
        attend_back_first,
        [shaped(tokens, 256), shaped(tokens, 384), shaped(8, 384, kind=f32)],
        *a_blocks, out_rows, query, key, value, mixed, logs, cosines, sines,
        scratch=grad32, flops=back_flops, exps=tokens * tokens, room=14,
    )
    pack_a = call(
        attention_grads_first,
        [shaped(4, 128, 640)] * 2,
        mixed, *a_blocks, hidden_a, grads_first,
        scratch=[pltpu.VMEM((256, width), bf16), pltpu.VMEM((256, 640), bf16)],
        flops=flops // 2, room=10,
    )
    grads_second, sums_r, p0, p1, p32 = call(
        attend_back_second,
        [shaped(tokens, 384), shaped(8, 384, kind=f32), part, part, two16],
        tie(d_out, *pack_a), grads_first, qkv, query, key, value, mixed, logs, cosines, sines,
        scratch=grad32 + [pltpu.VMEM((tokens, 768), bf16)],
        flops=back_flops, exps=tokens * tokens, room=14,
    )
    come_a = swap(pack_a[1], Y)
    p32 = tie(p32, come_u, layer_output)
    core_in, x_in = gather_sum(p1, p32)
    own_d, go_d = sum_near(tie(stay_d, p32), come_d)
    come_d = flip(go_d, 2)
    stay_u, go_u = sum_pairs(tie(pack_u[0], p32), come_u)
    (sums_a,) = call(gain_in_sums, [sums], p0, p1, p32, *blocks)
    pack_b = call(
        attention_grads_second,
        [shaped(4, 136, 384)] * 2,
        hidden_a, grads_second, sums_f, sums_b, sums_a, sums_u, sums_q, sums_r,
        flops=flops // 2, room=10,
    )
    x_in = tie(x_in, *pack_b, go_u)
    (d_rows,) = call(
        after_attention_back, [part], p0, core_in, x_in, own_rows, d_middle, vectors
    )
    input_gradient = lax.ppermute(d_rows, both, back_pairs)
    total_d = sum_far(tie(own_d, d_rows), come_d)
    own_u, go_u = sum_near(tie(stay_u, d_rows), flip(go_u, 1))
    stay_a, go_a = sum_pairs(tie(pack_a[0], d_rows), come_a)
    own_a, go_a = sum_near(stay_a, flip(go_a, 1))
    stay_b, go_b = sum_pairs(pack_b[0], swap(pack_b[1], Y))
    total_u = sum_far(own_u, flip(go_u, 2))
    own_b, go_b = sum_near(tie(stay_b, input_gradient), flip(go_b, 1))
    total_a = sum_far(own_a, flip(go_a, 2))
    total_b = sum_far(own_b, flip(go_b, 2))
    (g_down,) = call(unpack_down, [shaped(*down_weight.shape, kind=f32)], *gather_packs(total_d))
    (g_up,) = call(unpack_up, [shaped(*up_weight.shape, kind=f32)], *gather_packs(total_u))
    packs_a = gather_packs(total_a)
    packs_b = gather_packs(total_b)
    g_query, g_key, g_value, g_out, *small = call(
        unpack_attention,
        [part32] * 4 + [shaped(1, 256, kind=f32)] * 9 + [shaped(1, 1024, kind=f32)],
        *packs_a,
        *packs_b,
    )
    small = [item.reshape(-1) for item in small]
    input_gradient = input_gradient.astype(f32)
    return (
        layer_output,
        input_gradient,
        g_query,
        small[0],
        g_key,
        small[1],
        g_value,
        small[2],
        g_out,
        small[3],
        g_up,
        small[9],
        g_down,
        small[4],
        small[5],
        small[6],
        small[7],
        small[8],
    )


def solution(mesh):
    replicas, shards = mesh.shape["rep"], mesh.shape["shard"]
    fits = shards == 4 and replicas == 8 and HEADS % 16 == 0
    return jax.shard_map(
        fast_device if fits else general_device,
        mesh=mesh,
        in_specs=(
            P(("rep", "shard"), None),
            P("shard", None),
            P("shard"),
            P("shard", None),
            P("shard"),
            P("shard", None),
            P("shard"),
            P("shard", None),
            P("shard"),
            P("shard", None),
            P("shard"),
            P("shard", None),
            P("shard"),
            P("shard"),
            P("shard"),
            P("shard"),
            P("shard"),
            P(("rep", "shard"), None),
        ),
        out_specs=(
            P(("rep", "shard"), None),
            P(("rep", "shard"), None),
            P("shard", None),
            P("shard"),
            P("shard", None),
            P("shard"),
            P("shard", None),
            P("shard"),
            P("shard", None),
            P("shard"),
            P("shard", None),
            P("shard"),
            P("shard", None),
            P("shard"),
            P("shard"),
            P("shard"),
            P("shard"),
            P("shard"),
        ),
        check_vma=False,
    )
```

profile of v0, /device:TPU:0, one launch (start us, length us, event | category | flops | bytes accessed | tf_op | source)
XLA Modules:
  0.0 341.2 jit_solution(11664144571118792664)
XLA Ops:
  10.6 16.2 %collective-permute-start.1 = (bf16[256,1024]{1,0:T(8,128)(2,1)S(1)}, bf16[256,1024]{1,0:T(8,128)(2,1)S(1)}, u32[]{:S(2)}, u32[]{:S(2)}) collective-permute-start(bf16[256,1024]{1,0:T(8,128)(2,1)S(1)} %collective-permute-done.x0.rows_in), channel_id=1, source_target_pairs={{0,8},{4,12},{8,0},{12,4},{16,24},{20,28},{24,16},{28,20},{1,9},{5... | collective-permute-start | bytes 1572872 | tf_op jit(solution)/shard_map/ppermute | solution.py:473
  26.9 13.3 %collective-permute-done.5.z2 = bf16[144,1024]{1,0:T(8,128)(2,1)S(1)} collective-permute-done((bf16[144,1024]{1,0:T(8,128)(2,1)S(1)}, bf16[144,1024]{1,0:T(8,128)(2,1)S(1)}, u32[]{:S(2)}, u32[]{:S(2)}) %collective-permute-start.5) | collective-permute-done | bytes 294944 | tf_op jit(solution)/shard_map/ppermute | solution.py:483
  42.8 4.9 %collective-permute-done.6.z3 = bf16[144,1024]{1,0:T(8,128)(2,1)S(1)} collective-permute-done((bf16[144,1024]{1,0:T(8,128)(2,1)S(1)}, bf16[144,1024]{1,0:T(8,128)(2,1)S(1)}, u32[]{:S(2)}, u32[]{:S(2)}) %collective-permute-start.6) | collective-permute-done | bytes 294944 | tf_op jit(solution)/shard_map/ppermute | solution.py:483
  51.7 4.8 %collective-permute-done.7.y1 = bf16[144,1024]{1,0:T(8,128)(2,1)S(1)} collective-permute-done((bf16[144,1024]{1,0:T(8,128)(2,1)S(1)}, bf16[144,1024]{1,0:T(8,128)(2,1)S(1)}, u32[]{:S(2)}, u32[]{:S(2)}) %collective-permute-start.7) | collective-permute-done | bytes 294944 | tf_op jit(solution)/shard_map/ppermute | solution.py:473
  61.3 12.0 %attend.1 = (bf16[1024,256]{1,0:T(8,128)(2,1)S(1)}, bf16[1024,256]{1,0:T(8,128)(2,1)S(1)}, bf16[1024,256]{1,0:T(8,128)(2,1)S(1)}, bf16[1024,256]{1,0:T(8,128)(2,...) custom-call(bf16[256,1024]{1,0:T(8,128)(2,1)S(1)} %collective-permut, ...), custom_call_target="tpu_custom_call" | custom-call | flops 80530640 | bytes 361267 | tf_op jit(solution)/shard_map/attend/pallas_call | solution.py:535
  78.6 11.0 %collective-permute-done.17.d2 = bf16[128,1024]{1,0:T(8,128)(2,1)S(1)} collective-permute-done((bf16[128,1024]{1,0:T(8,128)(2,1)S(1)}, bf16[128,1024]{1,0:T(8,128)(2,1)S(1)}, u32[]{:S(2)}, u32[]{:S(2)}) %collective-permute-start.17) | collective-permute-done | bytes 262176 | tf_op jit(solution)/shard_map/ppermute | solution.py:483
  92.5 5.1 %collective-permute-done.18.d3 = bf16[128,1024]{1,0:T(8,128)(2,1)S(1)} collective-permute-done((bf16[128,1024]{1,0:T(8,128)(2,1)S(1)}, bf16[128,1024]{1,0:T(8,128)(2,1)S(1)}, u32[]{:S(2)}, u32[]{:S(2)}) %collective-permute-start.18) | collective-permute-done | bytes 262176 | tf_op jit(solution)/shard_map/ppermute | solution.py:483
  99.3 5.3 %collective-permute-done.14.x_in = bf16[256,1024]{1,0:T(8,128)(2,1)S(1)} collective-permute-done((bf16[256,1024]{1,0:T(8,128)(2,1)S(1)}, bf16[256,1024]{1,0:T(8,128)(2,1)S(1)}, u32[]{:S(2)}, u32[]{:S(2)}) %collective-permute-start.14) | collective-permute-done | bytes 524320 | tf_op jit(solution)/shard_map/ppermute | solution.py:473
  107.3 4.5 %collective-permute-start.21 = (bf16[256,1024]{1,0:T(8,128)(2,1)S(1)}, bf16[256,1024]{1,0:T(8,128)(2,1)S(1)}, u32[]{:S(2)}, u32[]{:S(2)}) collective-permute-start(bf16[256,1024]{1,0:T(8,128)(2,1)S(1)} %get-tuple-element.141.h0), channel_id=1, source_target_pairs={{0,8},{4,12},{8,0},{12,4},{16,24},{20,28},{24,16},{28,20},{1,9},{5... | collective-permute-start | bytes 1572872 | tf_op jit(solution)/shard_map/ppermute | solution.py:473
  111.8 4.4 %collective-permute-done.20.far_d = bf16[3,128,1024]{2,1,0:T(8,128)(2,1)S(1)} collective-permute-done((bf16[3,128,1024]{2,1,0:T(8,128)(2,1)S(1)}, bf16[3,128,1024]{2,1,0:T(8,128)(2,1)S(1)}, u32[]{:S(2)}, u32[]{:S(2)}) %collective-permute-start.20) | collective-permute-done | bytes 786464 | tf_op jit(solution)/shard_map/ppermute | solution.py:473
  116.2 5.7 %feed_first.1 = (bf16[1024,1024]{1,0:T(8,128)(2,1)S(1)}, bf16[1024,1024]{1,0:T(8,128)(2,1)S(1)}, f32[512,1024]{1,0:T(8,128)S(1)}, bf16[512,1024]{1,0:T(8,128)(2,...) custom-call(bf16[256,1024]{1,0:T(8,128)(2,1)S(1)} %get-tuple-element.141.h0, ...), custom_call_target="tpu_custom_call" | custom-call | flops 53687092 | bytes 341606 | tf_op jit(solution)/shard_map/feed_first/pallas_call | solution.py:535
  121.9 12.5 %collective-permute-done.21.h1 = bf16[256,1024]{1,0:T(8,128)(2,1)S(1)} collective-permute-done((bf16[256,1024]{1,0:T(8,128)(2,1)S(1)}, bf16[256,1024]{1,0:T(8,128)(2,1)S(1)}, u32[]{:S(2)}, u32[]{:S(2)}) %collective-permute-start.21) | collective-permute-done | bytes 524320 | tf_op jit(solution)/shard_map/ppermute | solution.py:473
  136.4 5.4 %feed_second.1 = (f32[512,1024]{1,0:T(8,128)S(1)}, bf16[512,1024]{1,0:T(8,128)(2,1)S(1)}, bf16[256,1024]{1,0:T(8,128)(2,1)S(1)}, bf16[512,1024]{1,0:T(8,128)(2,1)S(1)}) custom-call(bf16[256,1024]{1,0:T(8,128)(2,1)S(1)} %collective-permute-done.21.h1, bf16[256,1024]{1,0:T(8,128)(2,1)S(1)} %collective-permute-done.23.h3, ...), custom_call_target="tpu_custom_call" | custom-call | flops 53687092 | bytes 262963 | tf_op jit(solution)/shard_map/feed_second/pallas_call | solution.py:535
  147.3 12.2 %collective-permute-done.25.x_in = bf16[256,1024]{1,0:T(8,128)(2,1)S(1)} collective-permute-done((bf16[256,1024]{1,0:T(8,128)(2,1)S(1)}, bf16[256,1024]{1,0:T(8,128)(2,1)S(1)}, u32[]{:S(2)}, u32[]{:S(2)}) %collective-permute-start.25) | collective-permute-done | bytes 524320 | tf_op jit(solution)/shard_map/ppermute | solution.py:473
  163.1 5.8 %feed_back_first.1 = (bf16[512,1024]{1,0:T(8,128)(2,1)S(1)}, bf16[256,1024]{1,0:T(8,128)(2,1)S(1)}, bf16[256,1024]{1,0:T(8,128)(2,1)S(1)}, f32[8,1024]{1,0:T(8,128)S(1)}) custom-call(bf16[256,1024]{1,0:T(8,128)(2,1)S(1)} %get-tuple-element.152.m0, bf16[256,1024]{1,0:T(8,128)(2,1)S(1)} %collective-permute-done.26.m2, ...), custom_call_target="tpu_custom_call" | custom-call | flops 53687092 | bytes 236748 | tf_op jit(solution)/shard_map/feed_back_first/pallas_call | solution.py:535
  169.0 6.6 %collective-permute-done.27.m1 = bf16[256,1024]{1,0:T(8,128)(2,1)S(1)} collective-permute-done((bf16[256,1024]{1,0:T(8,128)(2,1)S(1)}, bf16[256,1024]{1,0:T(8,128)(2,1)S(1)}, u32[]{:S(2)}, u32[]{:S(2)}) %collective-permute-start.27) | collective-permute-done | bytes 524320 | tf_op jit(solution)/shard_map/ppermute | solution.py:473
  177.5 5.9 %feed_back_second.1 = (bf16[512,1024]{1,0:T(8,128)(2,1)S(1)}, bf16[256,1024]{1,0:T(8,128)(2,1)S(1)}, bf16[512,1024]{1,0:T(8,128)(2,1)S(1)}, f32[8,1024]{1,0:T(8,128)S(1)}) custom-call(bf16[256,1024]{1,0:T(8,128)(2,1)S(1)} %collective-permute-done.27.m1, bf16[256,1024]{1,0:T(8,128)(2,1)S(1)} %collective-permute-done.28.m3, ...), custom_call_target="tpu_custom_call" | custom-call | flops 53687092 | bytes 263782 | tf_op jit(solution)/shard_map/feed_back_second/pallas_call | solution.py:535
  205.4 12.0 %collective-permute-done.32.come = bf16[4,128,1024]{2,1,0:T(8,128)(2,1)S(1)} collective-permute-done((bf16[4,128,1024]{2,1,0:T(8,128)(2,1)S(1)}, bf16[4,128,1024]{2,1,0:T(8,128)(2,1)S(1)}, u32[]{:S(2)}, u32[]{:S(2)}) %collective-permute-start.32) | collective-permute-done | bytes 1048608 | tf_op jit(solution)/shard_map/ppermute | solution.py:473
  219.7 6.1 %attend_back_first.1 = (bf16[1024,256]{1,0:T(8,128)(2,1)S(1)}, bf16[1024,384]{1,0:T(8,128)(2,1)S(1)}, f32[8,384]{1,0:T(8,128)S(1)}) custom-call(bf16[256,1024]{1,0:T(8,128)(2,1)S(1)} %get-tuple-element.175.a0, bf16[256,1024]{1,0:T(8,128)(2,1)S(1)} %collective-permute-done.31.a1, bf16[256,1024]{1,0:T(8,128)(2,1)S(1)} %collective-permute-done.34.a2, ...), custom_call_target="tpu_custom_call" | custom-call | flops 60397976 | bytes 190361 | tf_op jit(solution)/shard_map/attend_back_first/pallas_call | solution.py:535
  228.7 7.4 %attend_back_second.1 = (bf16[1024,384]{1,0:T(8,128)(2,1)S(1)}, f32[8,384]{1,0:T(8,128)S(1)}, bf16[256,1024]{1,0:T(8,128)(2,1)S(1)}, bf16[256,1024]{1,0:T(8,128)(2,1)S(1)}, bf16[512,1024]{1,0:T(8,128)(2,1)S(1)}) custom-call(bf16[1024,256]{1,0:T(8,128)(2,1)S(1)} %get-tuple-element.191.d_out, bf16[1024,384]{1,0:T(8,128)(2,1)S(1)} %get-tuple-element.188.grads.before, ...), custom_call_target="tpu_custom_call" | custom-call | flops 60397976 | bytes 236236 | tf_op jit(solution)/shard_map/attend_back_second/pallas_call | solution.py:535
  246.1 7.4 %collective-permute-done.57.come = bf16[2,128,1024]{2,1,0:T(8,128)(2,1)S(1)} collective-permute-done((bf16[2,128,1024]{2,1,0:T(8,128)(2,1)S(1)}, bf16[2,128,1024]{2,1,0:T(8,128)(2,1)S(1)}, u32[]{:S(2)}, u32[]{:S(2)}) %collective-permute-start.57) | collective-permute-done | bytes 524320 | tf_op jit(solution)/shard_map/ppermute | solution.py:483
  260.3 9.7 %collective-permute-done.52.come = bf16[2,128,1024]{2,1,0:T(8,128)(2,1)S(1)} collective-permute-done((bf16[2,128,1024]{2,1,0:T(8,128)(2,1)S(1)}, bf16[2,128,1024]{2,1,0:T(8,128)(2,1)S(1)}, u32[]{:S(2)}, u32[]{:S(2)}) %collective-permute-start.52) | collective-permute-done | bytes 524320 | tf_op jit(solution)/shard_map/ppermute | solution.py:483
  275.2 8.5 %collective-permute-done.53 = bf16[128,1024]{1,0:T(8,128)(2,1)S(1)} collective-permute-done((bf16[128,1024]{1,0:T(8,128)(2,1)S(1)}, bf16[128,1024]{1,0:T(8,128)(2,1)S(1)}, u32[]{:S(2)}, u32[]{:S(2)}) %collective-permute-start.53) | collective-permute-done | bytes 262176 | tf_op jit(solution)/shard_map/ppermute | solution.py:483
  294.4 16.2 %collective-permute-done.42 = bf16[128,640]{1,0:T(8,128)(2,1)S(1)} collective-permute-done((bf16[128,640]{1,0:T(8,128)(2,1)S(1)}, bf16[128,640]{1,0:T(8,128)(2,1)S(1)}, u32[]{:S(2)}, u32[]{:S(2)}) %collective-permute-start.42) | collective-permute-done | bytes 163872 | tf_op jit(solution)/shard_map/ppermute | solution.py:483
  (190 shorter events, 136.9 us)
Async XLA Ops:
  10.6 31.7 %collective-permute-start.1 = (bf16[256,1024]{1,0:T(8,128)(2,1)S(1)}, bf16[256,1024]{1,0:T(8,128)(2,1)S(1)}, u32[]{:S(2)}, u32[]{:S(2)}) collective-permute-start(bf16[256,1024]{1,0:T(8,128)(2,1)S(1)} %collective-permute-done.x0.rows_in), channel_id=1, source_target_pairs={{0,8},{4,12},{8,0},{12,4},{16,24},{20,28},{24,16},{28,20},{1,9},{5... | collective-permute-start | bytes 1572872 | tf_op jit(solution)/shard_map/ppermute | solution.py:473
  42.3 19.0 %collective-permute-start.2 = (bf16[256,1024]{1,0:T(8,128)(2,1)S(1)}, bf16[256,1024]{1,0:T(8,128)(2,1)S(1)}, u32[]{:S(2)}, u32[]{:S(2)}) collective-permute-start(bf16[256,1024]{1,0:T(8,128)(2,1)S(1)} %collective-permute-done.x0.rows_in), channel_id=1, source_target_pairs={{0,4},{4,0},{8,12},{12,8},{16,20},{20,16},{24,28},{28,24},{1,5},{5... | collective-permute-start | bytes 1572872 | tf_op jit(solution)/shard_map/ppermute | solution.py:473
  42.3 19.0 %collective-permute-start.3 = (bf16[256,1024]{1,0:T(8,128)(2,1)S(1)}, bf16[256,1024]{1,0:T(8,128)(2,1)S(1)}, u32[]{:S(2)}, u32[]{:S(2)}) collective-permute-start(bf16[256,1024]{1,0:T(8,128)(2,1)S(1)} %collective-permute-done.1.x1), channel_id=1, source_target_pairs={{0,4},{4,0},{8,12},{12,8},{16,20},{20,16},{24,28},{28,24},{1,5},{5... | collective-permute-start | bytes 1572872 | tf_op jit(solution)/shard_map/ppermute | solution.py:473
  56.5 16.8 %collective-permute-start.10 = (bf16[128,1024]{1,0:T(8,128)(2,1)S(1)}, bf16[128,1024]{1,0:T(8,128)(2,1)S(1)}, u32[]{:S(2)}, u32[]{:S(2)}) collective-permute-start(bf16[128,1024]{1,0:T(8,128)(2,1)S(1)} %dynamic-slice_bitcast_fusion.2), channel_id=1, source_target_pairs={{0,1},{1,0},{2,3},{3,2},{4,5},{5,4},{6,7},{7,6},{8,9},{9,8},{10,11... | collective-permute-start | bytes 786440 | tf_op jit(solution)/shard_map/ppermute | solution.py:483
  73.4 16.2 %collective-permute-start.13 = (bf16[512,1024]{1,0:T(8,128)(2,1)S(1)}, bf16[512,1024]{1,0:T(8,128)(2,1)S(1)}, u32[]{:S(2)}, u32[]{:S(2)}) collective-permute-start(bf16[512,1024]{1,0:T(8,128)(2,1)S(1)} %get-tuple-element.135), channel_id=1, source_target_pairs={{0,4},{4,0},{8,12},{12,8},{16,20},{20,16},{24,28},{28,24},{1,5},{5... | collective-permute-start | bytes 3145736 | tf_op jit(solution)/shard_map/ppermute | solution.py:473
  77.0 22.3 %collective-permute-start.15 = (bf16[3,128,1024]{2,1,0:T(8,128)(2,1)S(1)}, bf16[3,128,1024]{2,1,0:T(8,128)(2,1)S(1)}, u32[]{:S(2)}, u32[]{:S(2)}) collective-permute-start(bf16[3,128,1024]{2,1,0:T(8,128)(2,1)S(1)} %pad_maximum_fusion.2), channel_id=1, source_target_pairs={{0,16},{4,20},{8,24},{12,28},{16,0},{20,4},{24,8},{28,12},{1,17},{... | collective-permute-start | bytes 2359304 | tf_op jit(solution)/shard_map/ppermute | solution.py:473
  97.7 18.5 %collective-permute-start.20 = (bf16[3,128,1024]{2,1,0:T(8,128)(2,1)S(1)}, bf16[3,128,1024]{2,1,0:T(8,128)(2,1)S(1)}, u32[]{:S(2)}, u32[]{:S(2)}) collective-permute-start(bf16[3,128,1024]{2,1,0:T(8,128)(2,1)S(1)} %pad_maximum_fusion.3), channel_id=1, source_target_pairs={{0,16},{4,20},{8,24},{12,28},{16,0},{20,4},{24,8},{28,12},{1,17},{... | collective-permute-start | bytes 2359304 | tf_op jit(solution)/shard_map/ppermute | solution.py:473
  107.3 27.1 %collective-permute-start.21 = (bf16[256,1024]{1,0:T(8,128)(2,1)S(1)}, bf16[256,1024]{1,0:T(8,128)(2,1)S(1)}, u32[]{:S(2)}, u32[]{:S(2)}) collective-permute-start(bf16[256,1024]{1,0:T(8,128)(2,1)S(1)} %get-tuple-element.141.h0), channel_id=1, source_target_pairs={{0,8},{4,12},{8,0},{12,4},{16,24},{20,28},{24,16},{28,20},{1,9},{5... | collective-permute-start | bytes 1572872 | tf_op jit(solution)/shard_map/ppermute | solution.py:473
  191.3 26.1 %collective-permute-start.32 = (bf16[4,128,1024]{2,1,0:T(8,128)(2,1)S(1)}, bf16[4,128,1024]{2,1,0:T(8,128)(2,1)S(1)}, u32[]{:S(2)}, u32[]{:S(2)}) collective-permute-start(bf16[4,128,1024]{2,1,0:T(8,128)(2,1)S(1)} %get-tuple-element.167), channel_id=1, source_target_pairs={{0,16},{4,20},{8,24},{12,28},{16,0},{20,4},{24,8},{28,12},{1,17},{... | collective-permute-start | bytes 3145736 | tf_op jit(solution)/shard_map/ppermute | solution.py:473
  203.9 34.9 %collective-permute-start.36 = (bf16[4,128,1024]{2,1,0:T(8,128)(2,1)S(1)}, bf16[4,128,1024]{2,1,0:T(8,128)(2,1)S(1)}, u32[]{:S(2)}, u32[]{:S(2)}) collective-permute-start(bf16[4,128,1024]{2,1,0:T(8,128)(2,1)S(1)} %get-tuple-element.170), channel_id=1, source_target_pairs={{0,16},{4,20},{8,24},{12,28},{16,0},{20,4},{24,8},{28,12},{1,17},{... | collective-permute-start | bytes 3145736 | tf_op jit(solution)/shard_map/ppermute | solution.py:473
  217.8 21.0 %collective-permute-start.33 = (bf16[256,1024]{1,0:T(8,128)(2,1)S(1)}, bf16[256,1024]{1,0:T(8,128)(2,1)S(1)}, u32[]{:S(2)}, u32[]{:S(2)}) collective-permute-start(bf16[256,1024]{1,0:T(8,128)(2,1)S(1)} %get-tuple-element.179), channel_id=1, source_target_pairs={{0,0},{8,1},{4,2},{12,3},{2,4},{10,5},{6,6},{14,7},{1,8},{9,9},{5,... | collective-permute-start | bytes 1572872 | tf_op jit(solution)/shard_map/ppermute | solution.py:1360
  241.6 17.3 %collective-permute-start.38 = (bf16[256,1024]{1,0:T(8,128)(2,1)S(1)}, bf16[256,1024]{1,0:T(8,128)(2,1)S(1)}, u32[]{:S(2)}, u32[]{:S(2)}) collective-permute-start(bf16[256,1024]{1,0:T(8,128)(2,1)S(1)} %add_convert_fusion), channel_id=1, source_target_pairs={{0,8},{4,12},{8,0},{12,4},{16,24},{20,28},{24,16},{28,20},{1,9},{5... | collective-permute-start | bytes 1572872 | tf_op jit(solution)/shard_map/ppermute | solution.py:473
  244.5 25.5 %collective-permute-start.52 = (bf16[2,128,1024]{2,1,0:T(8,128)(2,1)S(1)}, bf16[2,128,1024]{2,1,0:T(8,128)(2,1)S(1)}, u32[]{:S(2)}, u32[]{:S(2)}) collective-permute-start(bf16[2,128,1024]{2,1,0:T(8,128)(2,1)S(1)} %get-tuple-element.206), channel_id=1, source_target_pairs={{0,1},{1,0},{2,3},{3,2},{4,5},{5,4},{6,7},{7,6},{8,9},{9,8},{10,11... | collective-permute-start | bytes 1572872 | tf_op jit(solution)/shard_map/ppermute | solution.py:483
  244.5 29.9 %collective-permute-start.40 = (bf16[4,128,640]{2,1,0:T(8,128)(2,1)S(1)}, bf16[4,128,640]{2,1,0:T(8,128)(2,1)S(1)}, u32[]{:S(2)}, u32[]{:S(2)}) collective-permute-start(bf16[4,128,640]{2,1,0:T(8,128)(2,1)S(1)} %get-tuple-element.190), channel_id=1, source_target_pairs={{0,16},{4,20},{8,24},{12,28},{16,0},{20,4},{24,8},{28,12},{1,17},{... | collective-permute-start | bytes 1966088 | tf_op jit(solution)/shard_map/ppermute | solution.py:473
  253.6 18.1 %collective-permute-start.58 = (bf16[128,1024]{1,0:T(8,128)(2,1)S(1)}, bf16[128,1024]{1,0:T(8,128)(2,1)S(1)}, u32[]{:S(2)}, u32[]{:S(2)}) collective-permute-start(bf16[128,1024]{1,0:T(8,128)(2,1)S(1)} %get-tuple-element.236), channel_id=1, source_target_pairs={{0,2},{1,3},{2,0},{3,1},{4,6},{5,7},{6,4},{7,5},{8,10},{9,11},{10,... | collective-permute-start | bytes 786440 | tf_op jit(solution)/shard_map/ppermute | solution.py:483
  270.2 16.2 %collective-permute-start.46 = (bf16[4,136,384]{2,1,0:T(8,128)(2,1)S(1)}, bf16[4,136,384]{2,1,0:T(8,128)(2,1)S(1)}, u32[]{:S(2)}, u32[]{:S(2)}) collective-permute-start(bf16[4,136,384]{2,1,0:T(8,128)(2,1)S(1)} %get-tuple-element.204), channel_id=1, source_target_pairs={{0,16},{4,20},{8,24},{12,28},{16,0},{20,4},{24,8},{28,12},{1,17},{... | collective-permute-start | bytes 1253384 | tf_op jit(solution)/shard_map/ppermute | solution.py:473
  271.8 19.3 %collective-permute-start.59 = (bf16[128,1024]{1,0:T(8,128)(2,1)S(1)}, bf16[128,1024]{1,0:T(8,128)(2,1)S(1)}, u32[]{:S(2)}, u32[]{:S(2)}) collective-permute-start(bf16[128,1024]{1,0:T(8,128)(2,1)S(1)} %add_convert_fusion.4.own), channel_id=1, source_target_pairs={{0,8},{4,12},{8,0},{12,4},{16,24},{20,28},{24,16},{28,20},{1,9},{5... | collective-permute-start | bytes 786440 | tf_op jit(solution)/shard_map/ppermute | solution.py:473
  286.5 25.5 %collective-permute-start.47 = (bf16[2,136,384]{2,1,0:T(8,128)(2,1)S(1)}, bf16[2,136,384]{2,1,0:T(8,128)(2,1)S(1)}, u32[]{:S(2)}, u32[]{:S(2)}) collective-permute-start(bf16[2,136,384]{2,1,0:T(8,128)(2,1)S(1)} %get-tuple-element.216), channel_id=1, source_target_pairs={{0,1},{1,0},{2,3},{3,2},{4,5},{5,4},{6,7},{7,6},{8,9},{9,8},{10,11... | collective-permute-start | bytes 626696 | tf_op jit(solution)/shard_map/ppermute | solution.py:483
  286.6 25.5 %collective-permute-start.39 = (bf16[256,1024]{1,0:T(8,128)(2,1)S(1)}, bf16[256,1024]{1,0:T(8,128)(2,1)S(1)}, u32[]{:S(2)}, u32[]{:S(2)}) collective-permute-start(bf16[256,1024]{1,0:T(8,128)(2,1)S(1)} %after_attention_back.1), channel_id=1, source_target_pairs={{0,0},{8,1},{4,2},{12,3},{2,4},{10,5},{6,6},{14,7},{1,8},{9,9},{5,... | collective-permute-start | bytes 1572872 | tf_op jit(solution)/shard_map/ppermute | solution.py:1403
  289.1 21.5 %collective-permute-start.42 = (bf16[128,640]{1,0:T(8,128)(2,1)S(1)}, bf16[128,640]{1,0:T(8,128)(2,1)S(1)}, u32[]{:S(2)}, u32[]{:S(2)}) collective-permute-start(bf16[128,640]{1,0:T(8,128)(2,1)S(1)} %get-tuple-element.213), channel_id=1, source_target_pairs={{0,2},{1,3},{2,0},{3,1},{4,6},{5,7},{6,4},{7,5},{8,10},{9,11},{10,... | collective-permute-start | bytes 491528 | tf_op jit(solution)/shard_map/ppermute | solution.py:483
  291.2 26.5 %collective-permute-start.60 = (bf16[2,128,1024]{2,1,0:T(8,128)(2,1)S(1)}, bf16[2,128,1024]{2,1,0:T(8,128)(2,1)S(1)}, u32[]{:S(2)}, u32[]{:S(2)}) collective-permute-start(bf16[2,128,1024]{2,1,0:T(8,128)(2,1)S(1)} %pad_maximum_fusion.8), channel_id=1, source_target_pairs={{0,16},{4,20},{8,24},{12,28},{16,0},{20,4},{24,8},{28,12},{1,17},{... | collective-permute-start | bytes 1572872 | tf_op jit(solution)/shard_map/ppermute | solution.py:473
  292.8 25.0 %collective-permute-start.55 = (bf16[2,128,1024]{2,1,0:T(8,128)(2,1)S(1)}, bf16[2,128,1024]{2,1,0:T(8,128)(2,1)S(1)}, u32[]{:S(2)}, u32[]{:S(2)}) collective-permute-start(bf16[2,128,1024]{2,1,0:T(8,128)(2,1)S(1)} %pad_maximum_fusion.7), channel_id=1, source_target_pairs={{0,16},{4,20},{8,24},{12,28},{16,0},{20,4},{24,8},{28,12},{1,17},{... | collective-permute-start | bytes 1572872 | tf_op jit(solution)/shard_map/ppermute | solution.py:473
  317.7 18.0 %collective-permute-start.61 = (bf16[4,128,1024]{2,1,0:T(8,128)(2,1)S(1)}, bf16[4,128,1024]{2,1,0:T(8,128)(2,1)S(1)}, u32[]{:S(2)}, u32[]{:S(2)}) collective-permute-start(bf16[4,128,1024]{2,1,0:T(8,128)(2,1)S(1)} %pad_maximum_fusion.1), channel_id=1, source_target_pairs={{0,4},{4,0},{8,12},{12,8},{16,20},{20,16},{24,28},{28,24},{1,5},{5... | collective-permute-start | bytes 3145736 | tf_op jit(solution)/shard_map/ppermute | solution.py:473
  317.9 20.1 %collective-permute-start.56 = (bf16[4,128,1024]{2,1,0:T(8,128)(2,1)S(1)}, bf16[4,128,1024]{2,1,0:T(8,128)(2,1)S(1)}, u32[]{:S(2)}, u32[]{:S(2)}) collective-permute-start(bf16[4,128,1024]{2,1,0:T(8,128)(2,1)S(1)} %pad_maximum_fusion), channel_id=1, source_target_pairs={{0,4},{4,0},{8,12},{12,8},{16,20},{20,16},{24,28},{28,24},{1,5},{5... | collective-permute-start | bytes 3145736 | tf_op jit(solution)/shard_map/ppermute | solution.py:473
  (55 other events, 401.2 us)
where the time goes:
time: 341 us
  waiting for transfers between devices  171 us (50%)
  starting transfers between devices  79.7 us (23%)
  Pallas kernels  78.1 us (23%)
  other arithmetic  5.52 us (2%)
  local copies, waits for them, and re-layouts  5.25 us (2%)
    ppermute x41, waiting for transfers between devices, swap(): return lax.ppermute(values, 'rep', [(i, i ^ bit) for i in range(count)])  89.4 us
    ppermute x17, waiting for transfers between devices, flip(): return lax.ppermute(values, 'shard', [(i, i ^ bit) for i in range(count)])  81.9 us
    pallas_call x28, Pallas kernels, call(): pl.pallas_call(kernel, out_shape=tuple(outs), in_specs=[VMEM_SPEC] * len(...  77.8 us
    ppermute x41, starting transfers between devices, swap(): return lax.ppermute(values, 'rep', [(i, i ^ bit) for i in range(count)])  63.6 us
    ppermute x17, starting transfers between devices, flip(): return lax.ppermute(values, 'shard', [(i, i ^ bit) for i in range(count)])  11.6 us
  transfers between devices with their start and end apart: 62, of which 33 were waited for; matrix products, arithmetic and copies ran while one was open for 2% of the time, Pallas kernels for 18%

commit v1 on v0

--- a/solution.py
+++ b/solution.py
@@ -487,14 +487,14 @@
     pairs = []
     for rep in range(count):
         for z in range(GROUP):
-            there = (rep & ~3) | ((z & 1) << 1) | (z >> 1)
+            there = (rep & ~3) | (((z ^ rep) & 1) << 1) | (z >> 1)
             pairs.append((rep * GROUP + z, there * GROUP + ((rep >> 1) & 1) + 2 * (rep & 1)))
     return pairs
 
 
 def spot():
     rep, place = lax.axis_index("rep"), lax.axis_index("shard")
-    return rep & 3, place, rep >> 2, ((rep >> 1) & 1) + 2 * (rep & 1)
+    return rep & 3, place, rep >> 2, (((rep >> 1) & 1) ^ (place >> 1)) + 2 * (rep & 1)
 
 
 def aligned(index, size):
@@ -1174,11 +1174,11 @@
     return rounded(wide(own) + wide(come))
 
 
-def gather_packs(total):
+def gather_packs(total, *earlier):
     x_part = swap(total, X)
     two = jnp.stack([total, x_part])
     y_part = swap(two, Y)
-    return total, x_part, y_part, swap(jnp.concatenate([two, y_part]), CORE)
+    return total, x_part, y_part, swap(tie(jnp.concatenate([two, y_part]), *earlier), CORE)
 
 
 def fast_device(
@@ -1247,6 +1247,7 @@
     blocks = own_rows, x1, x2, swap(x1, CORE)
     far_a = far_pieces(near_a)
     near_u = near_pieces(up_packed, y_bit, *near_a)
+    cotangent = lax.ppermute(tie(layer_cotangent, *near_u), both, pairs)
     two16 = shaped(2 * rows, width)
     head_rows = shaped(tokens, 256)
     query, key, value, mixed, logs, hidden_a, qkv, out_rows, vectors, p0, p1, p32 = call(
@@ -1274,9 +1275,8 @@
     far_u = far_together(near_u)
     near_d = near_pieces(down_packed, y_bit, *near_u)
     core_in, x_in = gather_sum(p1, p32)
-    x_in = tie(x_in, far_u, *near_d)
+    x_in = tie(x_in, far_u, cotangent, *near_d)
     far_d = far_together(near_d)
-    cotangent = lax.ppermute(tie(layer_cotangent, *near_d), both, pairs)
     middle, hidden_own, normed_o, normed_f, inverses = call(
         after_attention,
         [part32, part, part32, part32, shaped(rows, 128, kind=f32)],
@@ -1297,7 +1297,7 @@
         h0, h2, up_packed, *near_u, far_u, down_packed, *near_d, far_d, vectors,
         flops=flops, room=10,
     )
-    h1 = tie(h1, p2, cotangent)
+    h1 = tie(h1, p2)
     h3 = swap(h1, CORE)
     before_b, after_b, p1, p32 = call(
         feed_second,
@@ -1319,6 +1319,8 @@
     )
     m1 = tie(m1, u_first)
     m3 = swap(m1, CORE)
+    layer_output = lax.ppermute(layer_output, both, back_pairs)
+    m3 = tie(m3, layer_output)
     packs = [shaped(4, 128, width)] * 2
     grad_flops = 2 * tokens * 1024 * 1024
     u_second, p1, p32, sums_u = call(
@@ -1357,7 +1359,6 @@
     stay_d, go_d = sum_pairs(tie(pack_d[0], d_branch), come_d)
     come_u = swap(pack_u[1], Y)
     a1 = tie(a1, go_d)
-    layer_output = lax.ppermute(tie(layer_output, a1), both, back_pairs)
     a3 = swap(a1, CORE)
     a_blocks = a0, a1, a2, a3
     come_d = flip(go_d, 1)
@@ -1384,7 +1385,7 @@
         flops=back_flops, exps=tokens * tokens, room=14,
     )
     come_a = swap(pack_a[1], Y)
-    p32 = tie(p32, come_u, layer_output)
+    p32 = tie(p32, come_u, come_d)
     core_in, x_in = gather_sum(p1, p32)
     own_d, go_d = sum_near(tie(stay_d, p32), come_d)
     come_d = flip(go_d, 2)
@@ -1413,7 +1414,7 @@
     (g_down,) = call(unpack_down, [shaped(*down_weight.shape, kind=f32)], *gather_packs(total_d))
     (g_up,) = call(unpack_up, [shaped(*up_weight.shape, kind=f32)], *gather_packs(total_u))
     packs_a = gather_packs(total_a)
-    packs_b = gather_packs(total_b)
+    packs_b = gather_packs(total_b, g_down)
     g_query, g_key, g_value, g_out, *small = call(
         unpack_attention,
         [part32] * 4 + [shaped(1, 256, kind=f32)] * 9 + [shaped(1, 1024, kind=f32)],

time: 341 us -> 333 us (0.977)
  waiting for transfers between devices: 171 us -> 161 us
    ppermute x17, starting transfers between devices: 11.6 us -> 20.6 us  [flip(): return lax.ppermute(values, 'shard', [(i, i ^ bit) for i in range(count)])]
    ppermute x41, starting transfers between devices: 63.6 us -> 56.5 us  [swap(): return lax.ppermute(values, 'rep', [(i, i ^ bit) for i in range(count)])]
    ppermute x17, waiting for transfers between devices: 81.9 us -> 75.1 us  [flip(): return lax.ppermute(values, 'shard', [(i, i ^ bit) for i in range(count)])]
  transfers between devices with their start and end apart: 62 -> 62, of which waited for: 33 -> 28; matrix products, arithmetic and copies ran while one was open for 2% -> 2% of each run, Pallas kernels for 18% -> 19%
where the time goes in v1:
time: 333 us
  waiting for transfers between devices  161 us (48%)
  starting transfers between devices  81.1 us (24%)
  Pallas kernels  78.4 us (24%)
  other arithmetic  5.52 us (2%)
  local copies, waits for them, and re-layouts  5.25 us (2%)
    ppermute x41, waiting for transfers between devices, swap(): return lax.ppermute(values, 'rep', [(i, i ^ bit) for i in range(count)])  86.3 us
    pallas_call x28, Pallas kernels, call(): pl.pallas_call(kernel, out_shape=tuple(outs), in_specs=[VMEM_SPEC] * len(...  78.1 us
    ppermute x17, waiting for transfers between devices, flip(): return lax.ppermute(values, 'shard', [(i, i ^ bit) for i in range(count)])  75.1 us
    ppermute x41, starting transfers between devices, swap(): return lax.ppermute(values, 'rep', [(i, i ^ bit) for i in range(count)])  56.5 us
    ppermute x17, starting transfers between devices, flip(): return lax.ppermute(values, 'shard', [(i, i ^ bit) for i in range(count)])  20.6 us
  transfers between devices with their start and end apart: 62, of which 28 were waited for; matrix products, arithmetic and copies ran while one was open for 2% of the time, Pallas kernels for 19%

profile of v1, /device:TPU:0, one launch (start us, length us, event | category | flops | bytes accessed | tf_op | source)
XLA Modules:
  0.0 333.0 jit_solution(7457013434454559801)
XLA Ops:
  10.6 16.2 %collective-permute-start.1 = (bf16[256,1024]{1,0:T(8,128)(2,1)S(1)}, bf16[256,1024]{1,0:T(8,128)(2,1)S(1)}, u32[]{:S(2)}, u32[]{:S(2)}) collective-permute-start(bf16[256,1024]{1,0:T(8,128)(2,1)S(1)} %collective-permute-done.x0.rows_in), channel_id=1, source_target_pairs={{0,8},{4,12},{8,0},{12,4},{16,24},{20,28},{24,16},{28,20},{1,9},{5... | collective-permute-start | bytes 1572872 | tf_op jit(solution)/shard_map/ppermute | solution.py:473
  26.9 13.3 %collective-permute-done.5.z2 = bf16[144,1024]{1,0:T(8,128)(2,1)S(1)} collective-permute-done((bf16[144,1024]{1,0:T(8,128)(2,1)S(1)}, bf16[144,1024]{1,0:T(8,128)(2,1)S(1)}, u32[]{:S(2)}, u32[]{:S(2)}) %collective-permute-start.5) | collective-permute-done | bytes 294944 | tf_op jit(solution)/shard_map/ppermute | solution.py:483
  42.9 4.8 %collective-permute-done.6.z3 = bf16[144,1024]{1,0:T(8,128)(2,1)S(1)} collective-permute-done((bf16[144,1024]{1,0:T(8,128)(2,1)S(1)}, bf16[144,1024]{1,0:T(8,128)(2,1)S(1)}, u32[]{:S(2)}, u32[]{:S(2)}) %collective-permute-start.6) | collective-permute-done | bytes 294944 | tf_op jit(solution)/shard_map/ppermute | solution.py:483
  51.8 4.8 %collective-permute-done.7.y1 = bf16[144,1024]{1,0:T(8,128)(2,1)S(1)} collective-permute-done((bf16[144,1024]{1,0:T(8,128)(2,1)S(1)}, bf16[144,1024]{1,0:T(8,128)(2,1)S(1)}, u32[]{:S(2)}, u32[]{:S(2)}) %collective-permute-start.7) | collective-permute-done | bytes 294944 | tf_op jit(solution)/shard_map/ppermute | solution.py:473
  60.9 12.0 %attend.1 = (bf16[1024,256]{1,0:T(8,128)(2,1)S(1)}, bf16[1024,256]{1,0:T(8,128)(2,1)S(1)}, bf16[1024,256]{1,0:T(8,128)(2,1)S(1)}, bf16[1024,256]{1,0:T(8,128)(2,...) custom-call(bf16[256,1024]{1,0:T(8,128)(2,1)S(1)} %collective-permut, ...), custom_call_target="tpu_custom_call" | custom-call | flops 80530640 | bytes 361267 | tf_op jit(solution)/shard_map/attend/pallas_call | solution.py:535
  79.1 10.1 %collective-permute-done.18.d2 = bf16[128,1024]{1,0:T(8,128)(2,1)S(1)} collective-permute-done((bf16[128,1024]{1,0:T(8,128)(2,1)S(1)}, bf16[128,1024]{1,0:T(8,128)(2,1)S(1)}, u32[]{:S(2)}, u32[]{:S(2)}) %collective-permute-start.18) | collective-permute-done | bytes 262176 | tf_op jit(solution)/shard_map/ppermute | solution.py:483
  92.4 8.8 %collective-permute-done.17.d1 = bf16[128,1024]{1,0:T(8,128)(2,1)S(1)} collective-permute-done((bf16[128,1024]{1,0:T(8,128)(2,1)S(1)}, bf16[128,1024]{1,0:T(8,128)(2,1)S(1)}, u32[]{:S(2)}, u32[]{:S(2)}) %collective-permute-start.17) | collective-permute-done | bytes 262176 | tf_op jit(solution)/shard_map/ppermute | solution.py:483
  101.3 10.9 %collective-permute-done.19.d3 = bf16[128,1024]{1,0:T(8,128)(2,1)S(1)} collective-permute-done((bf16[128,1024]{1,0:T(8,128)(2,1)S(1)}, bf16[128,1024]{1,0:T(8,128)(2,1)S(1)}, u32[]{:S(2)}, u32[]{:S(2)}) %collective-permute-start.19) | collective-permute-done | bytes 262176 | tf_op jit(solution)/shard_map/ppermute | solution.py:483
  117.7 7.8 %collective-permute-done.21.far_d = bf16[3,128,1024]{2,1,0:T(8,128)(2,1)S(1)} collective-permute-done((bf16[3,128,1024]{2,1,0:T(8,128)(2,1)S(1)}, bf16[3,128,1024]{2,1,0:T(8,128)(2,1)S(1)}, u32[]{:S(2)}, u32[]{:S(2)}) %collective-permute-start.21) | collective-permute-done | bytes 786464 | tf_op jit(solution)/shard_map/ppermute | solution.py:473
  125.5 5.7 %feed_first.1 = (bf16[1024,1024]{1,0:T(8,128)(2,1)S(1)}, bf16[1024,1024]{1,0:T(8,128)(2,1)S(1)}, f32[512,1024]{1,0:T(8,128)S(1)}, bf16[512,1024]{1,0:T(8,128)(2,...) custom-call(bf16[256,1024]{1,0:T(8,128)(2,1)S(1)} %get-tuple-element.143.h0, ...), custom_call_target="tpu_custom_call" | custom-call | flops 53687092 | bytes 341606 | tf_op jit(solution)/shard_map/feed_first/pallas_call | solution.py:535
  133.2 5.4 %feed_second.1 = (f32[512,1024]{1,0:T(8,128)S(1)}, bf16[512,1024]{1,0:T(8,128)(2,1)S(1)}, bf16[256,1024]{1,0:T(8,128)(2,1)S(1)}, bf16[512,1024]{1,0:T(8,128)(2,1)S(1)}) custom-call(bf16[256,1024]{1,0:T(8,128)(2,1)S(1)} %collective-permute-done.22.h1, bf16[256,1024]{1,0:T(8,128)(2,1)S(1)} %collective-permute-done.23.h3, ...), custom_call_target="tpu_custom_call" | custom-call | flops 53687092 | bytes 262963 | tf_op jit(solution)/shard_map/feed_second/pallas_call | solution.py:535
  143.7 12.2 %collective-permute-done.25.x_in = bf16[256,1024]{1,0:T(8,128)(2,1)S(1)} collective-permute-done((bf16[256,1024]{1,0:T(8,128)(2,1)S(1)}, bf16[256,1024]{1,0:T(8,128)(2,1)S(1)}, u32[]{:S(2)}, u32[]{:S(2)}) %collective-permute-start.25) | collective-permute-done | bytes 524320 | tf_op jit(solution)/shard_map/ppermute | solution.py:473
  160.1 5.9 %feed_back_first.1 = (bf16[512,1024]{1,0:T(8,128)(2,1)S(1)}, bf16[256,1024]{1,0:T(8,128)(2,1)S(1)}, bf16[256,1024]{1,0:T(8,128)(2,1)S(1)}, f32[8,1024]{1,0:T(8,128)S(1)}) custom-call(bf16[256,1024]{1,0:T(8,128)(2,1)S(1)} %get-tuple-element.153.m0, bf16[256,1024]{1,0:T(8,128)(2,1)S(1)} %collective-permute-done.27.m2, ...), custom_call_target="tpu_custom_call" | custom-call | flops 53687092 | bytes 236748 | tf_op jit(solution)/shard_map/feed_back_first/pallas_call | solution.py:535
  166.0 11.4 %collective-permute-done.28.m1 = bf16[256,1024]{1,0:T(8,128)(2,1)S(1)} collective-permute-done((bf16[256,1024]{1,0:T(8,128)(2,1)S(1)}, bf16[256,1024]{1,0:T(8,128)(2,1)S(1)}, u32[]{:S(2)}, u32[]{:S(2)}) %collective-permute-start.28) | collective-permute-done | bytes 524320 | tf_op jit(solution)/shard_map/ppermute | solution.py:473
  179.3 5.9 %feed_back_second.1 = (bf16[512,1024]{1,0:T(8,128)(2,1)S(1)}, bf16[256,1024]{1,0:T(8,128)(2,1)S(1)}, bf16[512,1024]{1,0:T(8,128)(2,1)S(1)}, f32[8,1024]{1,0:T(8,128)S(1)}) custom-call(bf16[256,1024]{1,0:T(8,128)(2,1)S(1)} %collective-permute-done.28.m1, bf16[256,1024]{1,0:T(8,128)(2,1)S(1)} %collective-permute-done.29.m3, ...), custom_call_target="tpu_custom_call" | custom-call | flops 53687092 | bytes 263782 | tf_op jit(solution)/shard_map/feed_back_second/pallas_call | solution.py:535
  198.1 4.2 %collective-permute-done.31.x_in = bf16[256,1024]{1,0:T(8,128)(2,1)S(1)} collective-permute-done((bf16[256,1024]{1,0:T(8,128)(2,1)S(1)}, bf16[256,1024]{1,0:T(8,128)(2,1)S(1)}, u32[]{:S(2)}, u32[]{:S(2)}) %collective-permute-start.31) | collective-permute-done | bytes 524320 | tf_op jit(solution)/shard_map/ppermute | solution.py:473
  207.4 12.0 %collective-permute-done.33.come = bf16[4,128,1024]{2,1,0:T(8,128)(2,1)S(1)} collective-permute-done((bf16[4,128,1024]{2,1,0:T(8,128)(2,1)S(1)}, bf16[4,128,1024]{2,1,0:T(8,128)(2,1)S(1)}, u32[]{:S(2)}, u32[]{:S(2)}) %collective-permute-start.33) | collective-permute-done | bytes 1048608 | tf_op jit(solution)/shard_map/ppermute | solution.py:473
  222.3 6.0 %attend_back_first.1 = (bf16[1024,256]{1,0:T(8,128)(2,1)S(1)}, bf16[1024,384]{1,0:T(8,128)(2,1)S(1)}, f32[8,384]{1,0:T(8,128)S(1)}) custom-call(bf16[256,1024]{1,0:T(8,128)(2,1)S(1)} %get-tuple-element.177.a0, bf16[256,1024]{1,0:T(8,128)(2,1)S(1)} %collective-permute-done.32.a1, bf16[256,1024]{1,0:T(8,128)(2,1)S(1)} %collective-permute-done.34.a2, ...), custom_call_target="tpu_custom_call" | custom-call | flops 60397976 | bytes 190361 | tf_op jit(solution)/shard_map/attend_back_first/pallas_call | solution.py:535
  231.3 7.6 %attend_back_second.1 = (bf16[1024,384]{1,0:T(8,128)(2,1)S(1)}, f32[8,384]{1,0:T(8,128)S(1)}, bf16[256,1024]{1,0:T(8,128)(2,1)S(1)}, bf16[256,1024]{1,0:T(8,128)(2,1)S(1)}, bf16[512,1024]{1,0:T(8,128)(2,1)S(1)}) custom-call(bf16[1024,256]{1,0:T(8,128)(2,1)S(1)} %get-tuple-element.192.d_out, bf16[1024,384]{1,0:T(8,128)(2,1)S(1)} %get-tuple-element.189.grads.before, ...), custom_call_target="tpu_custom_call" | custom-call | flops 60397976 | bytes 236236 | tf_op jit(solution)/shard_map/attend_back_second/pallas_call | solution.py:535
  259.0 5.4 %collective-permute-done.57.come = bf16[2,128,1024]{2,1,0:T(8,128)(2,1)S(1)} collective-permute-done((bf16[2,128,1024]{2,1,0:T(8,128)(2,1)S(1)}, bf16[2,128,1024]{2,1,0:T(8,128)(2,1)S(1)}, u32[]{:S(2)}, u32[]{:S(2)}) %collective-permute-start.57) | collective-permute-done | bytes 524320 | tf_op jit(solution)/shard_map/ppermute | solution.py:483
  270.8 7.9 %collective-permute-done.58 = bf16[128,1024]{1,0:T(8,128)(2,1)S(1)} collective-permute-done((bf16[128,1024]{1,0:T(8,128)(2,1)S(1)}, bf16[128,1024]{1,0:T(8,128)(2,1)S(1)}, u32[]{:S(2)}, u32[]{:S(2)}) %collective-permute-start.58) | collective-permute-done | bytes 262176 | tf_op jit(solution)/shard_map/ppermute | solution.py:483
  283.4 5.7 %collective-permute-done.59.x_part = bf16[128,1024]{1,0:T(8,128)(2,1)S(1)} collective-permute-done((bf16[128,1024]{1,0:T(8,128)(2,1)S(1)}, bf16[128,1024]{1,0:T(8,128)(2,1)S(1)}, u32[]{:S(2)}, u32[]{:S(2)}) %collective-permute-start.59) | collective-permute-done | bytes 262176 | tf_op jit(solution)/shard_map/ppermute | solution.py:473
  290.5 10.9 %collective-permute-done.43 = bf16[128,640]{1,0:T(8,128)(2,1)S(1)} collective-permute-done((bf16[128,640]{1,0:T(8,128)(2,1)S(1)}, bf16[128,640]{1,0:T(8,128)(2,1)S(1)}, u32[]{:S(2)}, u32[]{:S(2)}) %collective-permute-start.43) | collective-permute-done | bytes 163872 | tf_op jit(solution)/shard_map/ppermute | solution.py:483
  318.5 4.9 %collective-permute-done.51.y_part2 = bf16[2,136,384]{2,1,0:T(8,128)(2,1)S(1)} collective-permute-done((bf16[2,136,384]{2,1,0:T(8,128)(2,1)S(1)}, bf16[2,136,384]{2,1,0:T(8,128)(2,1)S(1)}, u32[]{:S(2)}, u32[]{:S(2)}) %collective-permute-start.51) | collective-permute-done | bytes 208928 | tf_op jit(solution)/shard_map/ppermute | solution.py:473
  (190 shorter events, 131.6 us)
Async XLA Ops:
  10.6 31.8 %collective-permute-start.1 = (bf16[256,1024]{1,0:T(8,128)(2,1)S(1)}, bf16[256,1024]{1,0:T(8,128)(2,1)S(1)}, u32[]{:S(2)}, u32[]{:S(2)}) collective-permute-start(bf16[256,1024]{1,0:T(8,128)(2,1)S(1)} %collective-permute-done.x0.rows_in), channel_id=1, source_target_pairs={{0,8},{4,12},{8,0},{12,4},{16,24},{20,28},{24,16},{28,20},{1,9},{5... | collective-permute-start | bytes 1572872 | tf_op jit(solution)/shard_map/ppermute | solution.py:473
  42.4 18.5 %collective-permute-start.2 = (bf16[256,1024]{1,0:T(8,128)(2,1)S(1)}, bf16[256,1024]{1,0:T(8,128)(2,1)S(1)}, u32[]{:S(2)}, u32[]{:S(2)}) collective-permute-start(bf16[256,1024]{1,0:T(8,128)(2,1)S(1)} %collective-permute-done.x0.rows_in), channel_id=1, source_target_pairs={{0,4},{4,0},{8,12},{12,8},{16,20},{20,16},{24,28},{28,24},{1,5},{5... | collective-permute-start | bytes 1572872 | tf_op jit(solution)/shard_map/ppermute | solution.py:473
  42.4 18.5 %collective-permute-start.3 = (bf16[256,1024]{1,0:T(8,128)(2,1)S(1)}, bf16[256,1024]{1,0:T(8,128)(2,1)S(1)}, u32[]{:S(2)}, u32[]{:S(2)}) collective-permute-start(bf16[256,1024]{1,0:T(8,128)(2,1)S(1)} %collective-permute-done.1.x1), channel_id=1, source_target_pairs={{0,4},{4,0},{8,12},{12,8},{16,20},{20,16},{24,28},{28,24},{1,5},{5... | collective-permute-start | bytes 1572872 | tf_op jit(solution)/shard_map/ppermute | solution.py:473
  56.6 16.4 %collective-permute-start.10 = (bf16[128,1024]{1,0:T(8,128)(2,1)S(1)}, bf16[128,1024]{1,0:T(8,128)(2,1)S(1)}, u32[]{:S(2)}, u32[]{:S(2)}) collective-permute-start(bf16[128,1024]{1,0:T(8,128)(2,1)S(1)} %dynamic-slice_bitcast_fusion.2), channel_id=1, source_target_pairs={{0,1},{1,0},{2,3},{3,2},{4,5},{5,4},{6,7},{7,6},{8,9},{9,8},{10,11... | collective-permute-start | bytes 786440 | tf_op jit(solution)/shard_map/ppermute | solution.py:483
  76.5 24.8 %collective-permute-start.17 = (bf16[128,1024]{1,0:T(8,128)(2,1)S(1)}, bf16[128,1024]{1,0:T(8,128)(2,1)S(1)}, u32[]{:S(2)}, u32[]{:S(2)}) collective-permute-start(bf16[128,1024]{1,0:T(8,128)(2,1)S(1)} %dynamic-slice_bitcast_fusion.1), channel_id=1, source_target_pairs={{0,1},{1,0},{2,3},{3,2},{4,5},{5,4},{6,7},{7,6},{8,9},{9,8},{10,11... | collective-permute-start | bytes 786440 | tf_op jit(solution)/shard_map/ppermute | solution.py:483
  76.5 37.3 %collective-permute-start.16 = (bf16[256,1024]{1,0:T(8,128)(2,1)S(1)}, bf16[256,1024]{1,0:T(8,128)(2,1)S(1)}, u32[]{:S(2)}, u32[]{:S(2)}) collective-permute-start(bf16[256,1024]{1,0:T(8,128)(2,1)S(1)} %copy-done.16), channel_id=1, source_target_pairs={{0,0},{1,8},{2,4},{3,12},{4,10},{5,2},{6,14},{7,6},{8,1},{9,9},{10... | collective-permute-start | bytes 1572872 | tf_op jit(solution)/shard_map/ppermute | solution.py:1250
  77.5 36.3 %collective-permute-start.15 = (bf16[3,128,1024]{2,1,0:T(8,128)(2,1)S(1)}, bf16[3,128,1024]{2,1,0:T(8,128)(2,1)S(1)}, u32[]{:S(2)}, u32[]{:S(2)}) collective-permute-start(bf16[3,128,1024]{2,1,0:T(8,128)(2,1)S(1)} %pad_maximum_fusion.2), channel_id=1, source_target_pairs={{0,16},{4,20},{8,24},{12,28},{16,0},{20,4},{24,8},{28,12},{1,17},{... | collective-permute-start | bytes 2359304 | tf_op jit(solution)/shard_map/ppermute | solution.py:473
  89.2 23.0 %collective-permute-start.19 = (bf16[128,1024]{1,0:T(8,128)(2,1)S(1)}, bf16[128,1024]{1,0:T(8,128)(2,1)S(1)}, u32[]{:S(2)}, u32[]{:S(2)}) collective-permute-start(bf16[128,1024]{1,0:T(8,128)(2,1)S(1)} %collective-permute-done.18.d2), channel_id=1, source_target_pairs={{0,1},{1,0},{2,3},{3,2},{4,5},{5,4},{6,7},{7,6},{8,9},{9,8},{10,11... | collective-permute-start | bytes 786440 | tf_op jit(solution)/shard_map/ppermute | solution.py:483
  89.4 24.5 %collective-permute-start.14 = (bf16[256,1024]{1,0:T(8,128)(2,1)S(1)}, bf16[256,1024]{1,0:T(8,128)(2,1)S(1)}, u32[]{:S(2)}, u32[]{:S(2)}) collective-permute-start(bf16[256,1024]{1,0:T(8,128)(2,1)S(1)} %add_convert_fusion.3), channel_id=1, source_target_pairs={{0,8},{4,12},{8,0},{12,4},{16,24},{20,28},{24,16},{28,20},{1,9},{5... | collective-permute-start | bytes 1572872 | tf_op jit(solution)/shard_map/ppermute | solution.py:473
  157.6 19.8 %collective-permute-start.28 = (bf16[256,1024]{1,0:T(8,128)(2,1)S(1)}, bf16[256,1024]{1,0:T(8,128)(2,1)S(1)}, u32[]{:S(2)}, u32[]{:S(2)}) collective-permute-start(bf16[256,1024]{1,0:T(8,128)(2,1)S(1)} %get-tuple-element.153.m0), channel_id=1, source_target_pairs={{0,8},{4,12},{8,0},{12,4},{16,24},{20,28},{24,16},{28,20},{1,9},{5... | collective-permute-start | bytes 1572872 | tf_op jit(solution)/shard_map/ppermute | solution.py:473
  159.4 18.0 %collective-permute-start.26 = (bf16[256,1024]{1,0:T(8,128)(2,1)S(1)}, bf16[256,1024]{1,0:T(8,128)(2,1)S(1)}, u32[]{:S(2)}, u32[]{:S(2)}) collective-permute-start(bf16[256,1024]{1,0:T(8,128)(2,1)S(1)} %get-tuple-element.152), channel_id=1, source_target_pairs={{0,0},{8,1},{4,2},{12,3},{10,4},{2,5},{14,6},{6,7},{1,8},{9,9},{5,... | collective-permute-start | bytes 1572872 | tf_op jit(solution)/shard_map/ppermute | solution.py:1322
  193.3 26.1 %collective-permute-start.33 = (bf16[4,128,1024]{2,1,0:T(8,128)(2,1)S(1)}, bf16[4,128,1024]{2,1,0:T(8,128)(2,1)S(1)}, u32[]{:S(2)}, u32[]{:S(2)}) collective-permute-start(bf16[4,128,1024]{2,1,0:T(8,128)(2,1)S(1)} %get-tuple-element.169), channel_id=1, source_target_pairs={{0,16},{4,20},{8,24},{12,28},{16,0},{20,4},{24,8},{28,12},{1,17},{... | collective-permute-start | bytes 3145736 | tf_op jit(solution)/shard_map/ppermute | solution.py:473
  205.9 34.9 %collective-permute-start.36 = (bf16[4,128,1024]{2,1,0:T(8,128)(2,1)S(1)}, bf16[4,128,1024]{2,1,0:T(8,128)(2,1)S(1)}, u32[]{:S(2)}, u32[]{:S(2)}) collective-permute-start(bf16[4,128,1024]{2,1,0:T(8,128)(2,1)S(1)} %get-tuple-element.172), channel_id=1, source_target_pairs={{0,16},{4,20},{8,24},{12,28},{16,0},{20,4},{24,8},{28,12},{1,17},{... | collective-permute-start | bytes 3145736 | tf_op jit(solution)/shard_map/ppermute | solution.py:473
  219.8 21.0 %collective-permute-start.37 = (bf16[2,128,1024]{2,1,0:T(8,128)(2,1)S(1)}, bf16[2,128,1024]{2,1,0:T(8,128)(2,1)S(1)}, u32[]{:S(2)}, u32[]{:S(2)}) collective-permute-start(bf16[2,128,1024]{2,1,0:T(8,128)(2,1)S(1)} %get-tuple-element.179), channel_id=1, source_target_pairs={{0,1},{1,0},{2,3},{3,2},{4,5},{5,4},{6,7},{7,6},{8,9},{9,8},{10,11... | collective-permute-start | bytes 1572872 | tf_op jit(solution)/shard_map/ppermute | solution.py:483
  244.3 20.1 %collective-permute-start.57 = (bf16[2,128,1024]{2,1,0:T(8,128)(2,1)S(1)}, bf16[2,128,1024]{2,1,0:T(8,128)(2,1)S(1)}, u32[]{:S(2)}, u32[]{:S(2)}) collective-permute-start(bf16[2,128,1024]{2,1,0:T(8,128)(2,1)S(1)} %get-tuple-element.207), channel_id=1, source_target_pairs={{0,1},{1,0},{2,3},{3,2},{4,5},{5,4},{6,7},{7,6},{8,9},{9,8},{10,11... | collective-permute-start | bytes 1572872 | tf_op jit(solution)/shard_map/ppermute | solution.py:483
  246.8 21.3 %collective-permute-start.41 = (bf16[4,128,640]{2,1,0:T(8,128)(2,1)S(1)}, bf16[4,128,640]{2,1,0:T(8,128)(2,1)S(1)}, u32[]{:S(2)}, u32[]{:S(2)}) collective-permute-start(bf16[4,128,640]{2,1,0:T(8,128)(2,1)S(1)} %get-tuple-element.191), channel_id=1, source_target_pairs={{0,16},{4,20},{8,24},{12,28},{16,0},{20,4},{24,8},{28,12},{1,17},{... | collective-permute-start | bytes 1966088 | tf_op jit(solution)/shard_map/ppermute | solution.py:473
  248.4 17.7 %collective-permute-start.52 = (bf16[128,1024]{1,0:T(8,128)(2,1)S(1)}, bf16[128,1024]{1,0:T(8,128)(2,1)S(1)}, u32[]{:S(2)}, u32[]{:S(2)}) collective-permute-start(bf16[128,1024]{1,0:T(8,128)(2,1)S(1)} %get-tuple-element.224), channel_id=1, source_target_pairs={{0,2},{1,3},{2,0},{3,1},{4,6},{5,7},{6,4},{7,5},{8,10},{9,11},{10,... | collective-permute-start | bytes 786440 | tf_op jit(solution)/shard_map/ppermute | solution.py:483
  266.6 23.1 %collective-permute-start.47 = (bf16[4,136,384]{2,1,0:T(8,128)(2,1)S(1)}, bf16[4,136,384]{2,1,0:T(8,128)(2,1)S(1)}, u32[]{:S(2)}, u32[]{:S(2)}) collective-permute-start(bf16[4,136,384]{2,1,0:T(8,128)(2,1)S(1)} %get-tuple-element.205), channel_id=1, source_target_pairs={{0,16},{4,20},{8,24},{12,28},{16,0},{20,4},{24,8},{28,12},{1,17},{... | collective-permute-start | bytes 1253384 | tf_op jit(solution)/shard_map/ppermute | solution.py:473
  279.7 25.6 %collective-permute-start.40 = (bf16[256,1024]{1,0:T(8,128)(2,1)S(1)}, bf16[256,1024]{1,0:T(8,128)(2,1)S(1)}, u32[]{:S(2)}, u32[]{:S(2)}) collective-permute-start(bf16[256,1024]{1,0:T(8,128)(2,1)S(1)} %after_attention_back.1), channel_id=1, source_target_pairs={{0,0},{8,1},{4,2},{12,3},{10,4},{2,5},{14,6},{6,7},{1,8},{9,9},{5,... | collective-permute-start | bytes 1572872 | tf_op jit(solution)/shard_map/ppermute | solution.py:1404
  280.4 25.0 %collective-permute-start.54 = (bf16[2,128,1024]{2,1,0:T(8,128)(2,1)S(1)}, bf16[2,128,1024]{2,1,0:T(8,128)(2,1)S(1)}, u32[]{:S(2)}, u32[]{:S(2)}) collective-permute-start(bf16[2,128,1024]{2,1,0:T(8,128)(2,1)S(1)} %pad_maximum_fusion.7), channel_id=1, source_target_pairs={{0,16},{4,20},{8,24},{12,28},{16,0},{20,4},{24,8},{28,12},{1,17},{... | collective-permute-start | bytes 1572872 | tf_op jit(solution)/shard_map/ppermute | solution.py:473
  282.1 19.3 %collective-permute-start.43 = (bf16[128,640]{1,0:T(8,128)(2,1)S(1)}, bf16[128,640]{1,0:T(8,128)(2,1)S(1)}, u32[]{:S(2)}, u32[]{:S(2)}) collective-permute-start(bf16[128,640]{1,0:T(8,128)(2,1)S(1)} %get-tuple-element.214), channel_id=1, source_target_pairs={{0,2},{1,3},{2,0},{3,1},{4,6},{5,7},{6,4},{7,5},{8,10},{9,11},{10,... | collective-permute-start | bytes 491528 | tf_op jit(solution)/shard_map/ppermute | solution.py:483
  289.1 21.1 %collective-permute-start.60 = (bf16[2,128,1024]{2,1,0:T(8,128)(2,1)S(1)}, bf16[2,128,1024]{2,1,0:T(8,128)(2,1)S(1)}, u32[]{:S(2)}, u32[]{:S(2)}) collective-permute-start(bf16[2,128,1024]{2,1,0:T(8,128)(2,1)S(1)} %pad_maximum_fusion.8), channel_id=1, source_target_pairs={{0,16},{4,20},{8,24},{12,28},{16,0},{20,4},{24,8},{28,12},{1,17},{... | collective-permute-start | bytes 1572872 | tf_op jit(solution)/shard_map/ppermute | solution.py:473
  305.6 17.9 %collective-permute-start.55 = (bf16[4,128,1024]{2,1,0:T(8,128)(2,1)S(1)}, bf16[4,128,1024]{2,1,0:T(8,128)(2,1)S(1)}, u32[]{:S(2)}, u32[]{:S(2)}) collective-permute-start(bf16[4,128,1024]{2,1,0:T(8,128)(2,1)S(1)} %pad_maximum_fusion), channel_id=1, source_target_pairs={{0,4},{4,0},{8,12},{12,8},{16,20},{20,16},{24,28},{28,24},{1,5},{5... | collective-permute-start | bytes 3145736 | tf_op jit(solution)/shard_map/ppermute | solution.py:473
  310.3 16.5 %collective-permute-start.61 = (bf16[4,128,1024]{2,1,0:T(8,128)(2,1)S(1)}, bf16[4,128,1024]{2,1,0:T(8,128)(2,1)S(1)}, u32[]{:S(2)}, u32[]{:S(2)}) collective-permute-start(bf16[4,128,1024]{2,1,0:T(8,128)(2,1)S(1)} %pad_maximum_fusion.1), channel_id=1, source_target_pairs={{0,4},{4,0},{8,12},{12,8},{16,20},{20,16},{24,28},{28,24},{1,5},{5... | collective-permute-start | bytes 3145736 | tf_op jit(solution)/shard_map/ppermute | solution.py:473
  (55 other events, 441.2 us)

commit v2 on v1

--- a/solution.py
+++ b/solution.py
@@ -1242,11 +1242,11 @@
     near_a = near_pieces(packed, y_bit)
     cosines, sines = rope_tables(tokens, 64)
     up_packed, down_packed = call_pack_feed(up_weight, down_weight)
-    own_rows = tie(own_rows, packed, cosines, sines, up_packed)
+    own_rows = tie(own_rows, near_a[1], cosines, sines, up_packed)
     x1, x2 = spread(own_rows)
     blocks = own_rows, x1, x2, swap(x1, CORE)
     far_a = far_pieces(near_a)
-    near_u = near_pieces(up_packed, y_bit, *near_a)
+    near_u = near_pieces(up_packed, y_bit, *near_a, direct=True)
     cotangent = lax.ppermute(tie(layer_cotangent, *near_u), both, pairs)
     two16 = shaped(2 * rows, width)
     head_rows = shaped(tokens, 256)

time: 333 us -> 335 us (level)
  starting transfers between devices: 81.1 us -> 53.6 us
  waiting for transfers between devices: 161 us -> 182 us
  local copies, waits for them, and re-layouts: 5.25 us -> 13.2 us
    ppermute x41, starting transfers between devices: 56.5 us -> 32.1 us  [swap(): return lax.ppermute(values, 'rep', [(i, i ^ bit) for i in range(count)])]
    ppermute x41, waiting for transfers between devices: 86.3 us -> 104 us  [swap(): return lax.ppermute(values, 'rep', [(i, i ^ bit) for i in range(count)])]
    unnamed x35, local copies, waits for them, and re-layouts: 5.19 us -> 13.1 us
  transfers between devices with their start and end apart: 62 -> 62, of which waited for: 28 -> 32; matrix products, arithmetic and copies ran while one was open for 2% -> 2% of each run, Pallas kernels for 19% -> 19%
where the time goes in v2:
time: 335 us; the launch traced here: 334 us
  waiting for transfers between devices  182 us (54%)
  Pallas kernels  78.3 us (23%)
  starting transfers between devices  53.6 us (16%)
  local copies, waits for them, and re-layouts  13.2 us (4%)
  other arithmetic  5.52 us (2%)
    ppermute x41, waiting for transfers between devices, swap(): return lax.ppermute(values, 'rep', [(i, i ^ bit) for i in range(count)])  104 us
    ppermute x17, waiting for transfers between devices, flip(): return lax.ppermute(values, 'shard', [(i, i ^ bit) for i in range(count)])  78.5 us
    pallas_call x28, Pallas kernels, call(): pl.pallas_call(kernel, out_shape=tuple(outs), in_specs=[VMEM_SPEC] * len(...  78.1 us
    ppermute x41, starting transfers between devices, swap(): return lax.ppermute(values, 'rep', [(i, i ^ bit) for i in range(count)])  32.1 us
    ppermute x17, starting transfers between devices, flip(): return lax.ppermute(values, 'shard', [(i, i ^ bit) for i in range(count)])  17.4 us
    unnamed x35, local copies, waits for them, and re-layouts  13.1 us
  transfers between devices with their start and end apart: 62, of which 32 were waited for; matrix products, arithmetic and copies ran while one was open for 2% of the time, Pallas kernels for 19%

profile of v2, /device:TPU:0, one launch (start us, length us, event | category | flops | bytes accessed | tf_op | source)
XLA Modules:
  0.0 334.2 jit_solution(14275925339011260526)
XLA Ops:
  14.0 4.3 %collective-permute-start.1 = (bf16[144,1024]{1,0:T(8,128)(2,1)S(1)}, bf16[144,1024]{1,0:T(8,128)(2,1)S(1)}, u32[]{:S(2)}, u32[]{:S(2)}) collective-permute-start(bf16[144,1024]{1,0:T(8,128)(2,1)S(1)} %dynamic-slice_bitcast_fusion), channel_id=1, source_target_pairs={{0,2},{1,3},{2,0},{3,1},{4,6},{5,7},{6,4},{7,5},{8,10},{9,11},{10,... | collective-permute-start | bytes 884744 | tf_op jit(solution)/shard_map/ppermute | solution.py:483
  22.9 7.7 %collective-permute-done.1.z2 = bf16[144,1024]{1,0:T(8,128)(2,1)S(1)} collective-permute-done((bf16[144,1024]{1,0:T(8,128)(2,1)S(1)}, bf16[144,1024]{1,0:T(8,128)(2,1)S(1)}, u32[]{:S(2)}, u32[]{:S(2)}) %collective-permute-start.1) | collective-permute-done | bytes 294944 | tf_op jit(solution)/shard_map/ppermute | solution.py:483
  30.7 5.1 %collective-permute-start.2 = (bf16[256,1024]{1,0:T(8,128)(2,1)S(1)}, bf16[256,1024]{1,0:T(8,128)(2,1)S(1)}, u32[]{:S(2)}, u32[]{:S(2)}) collective-permute-start(bf16[256,1024]{1,0:T(8,128)(2,1)S(1)} %collective-permute-done.x0.rows_in), channel_id=1, source_target_pairs={{0,8},{4,12},{8,0},{12,4},{16,24},{20,28},{24,16},{28,20},{1,9},{5... | collective-permute-start | bytes 1572872 | tf_op jit(solution)/shard_map/ppermute | solution.py:473
  37.8 7.9 %collective-permute-done.5.z1 = bf16[144,1024]{1,0:T(8,128)(2,1)S(1)} collective-permute-done((bf16[144,1024]{1,0:T(8,128)(2,1)S(1)}, bf16[144,1024]{1,0:T(8,128)(2,1)S(1)}, u32[]{:S(2)}, u32[]{:S(2)}) %collective-permute-start.5) | collective-permute-done | bytes 294944 | tf_op jit(solution)/shard_map/ppermute | solution.py:483
  64.5 12.0 %attend.1 = (bf16[1024,256]{1,0:T(8,128)(2,1)S(1)}, bf16[1024,256]{1,0:T(8,128)(2,1)S(1)}, bf16[1024,256]{1,0:T(8,128)(2,1)S(1)}, bf16[1024,256]{1,0:T(8,128)(2,...) custom-call(bf16[256,1024]{1,0:T(8,128)(2,1)S(1)} %collective-permut, ...), custom_call_target="tpu_custom_call" | custom-call | flops 80530640 | bytes 361267 | tf_op jit(solution)/shard_map/attend/pallas_call | solution.py:535
  81.3 11.3 %collective-permute-done.18.d2 = bf16[128,1024]{1,0:T(8,128)(2,1)S(1)} collective-permute-done((bf16[128,1024]{1,0:T(8,128)(2,1)S(1)}, bf16[128,1024]{1,0:T(8,128)(2,1)S(1)}, u32[]{:S(2)}, u32[]{:S(2)}) %collective-permute-start.18) | collective-permute-done | bytes 262176 | tf_op jit(solution)/shard_map/ppermute | solution.py:483
  93.1 21.6 %collective-permute-done.19.d3 = bf16[128,1024]{1,0:T(8,128)(2,1)S(1)} collective-permute-done((bf16[128,1024]{1,0:T(8,128)(2,1)S(1)}, bf16[128,1024]{1,0:T(8,128)(2,1)S(1)}, u32[]{:S(2)}, u32[]{:S(2)}) %collective-permute-start.19) | collective-permute-done | bytes 262176 | tf_op jit(solution)/shard_map/ppermute | solution.py:483
  119.1 9.9 %collective-permute-done.21.far_d = bf16[3,128,1024]{2,1,0:T(8,128)(2,1)S(1)} collective-permute-done((bf16[3,128,1024]{2,1,0:T(8,128)(2,1)S(1)}, bf16[3,128,1024]{2,1,0:T(8,128)(2,1)S(1)}, u32[]{:S(2)}, u32[]{:S(2)}) %collective-permute-start.21) | collective-permute-done | bytes 786464 | tf_op jit(solution)/shard_map/ppermute | solution.py:473
  129.0 5.7 %feed_first.1 = (bf16[1024,1024]{1,0:T(8,128)(2,1)S(1)}, bf16[1024,1024]{1,0:T(8,128)(2,1)S(1)}, f32[512,1024]{1,0:T(8,128)S(1)}, bf16[512,1024]{1,0:T(8,128)(2,...) custom-call(bf16[256,1024]{1,0:T(8,128)(2,1)S(1)} %get-tuple-element.143.h0, ...), custom_call_target="tpu_custom_call" | custom-call | flops 53687092 | bytes 341606 | tf_op jit(solution)/shard_map/feed_first/pallas_call | solution.py:535
  136.7 5.4 %feed_second.1 = (f32[512,1024]{1,0:T(8,128)S(1)}, bf16[512,1024]{1,0:T(8,128)(2,1)S(1)}, bf16[256,1024]{1,0:T(8,128)(2,1)S(1)}, bf16[512,1024]{1,0:T(8,128)(2,1)S(1)}) custom-call(bf16[256,1024]{1,0:T(8,128)(2,1)S(1)} %collective-permute-done.22.h1, bf16[256,1024]{1,0:T(8,128)(2,1)S(1)} %collective-permute-done.23.h3, ...), custom_call_target="tpu_custom_call" | custom-call | flops 53687092 | bytes 262963 | tf_op jit(solution)/shard_map/feed_second/pallas_call | solution.py:535
  145.2 14.0 %collective-permute-done.25.x_in = bf16[256,1024]{1,0:T(8,128)(2,1)S(1)} collective-permute-done((bf16[256,1024]{1,0:T(8,128)(2,1)S(1)}, bf16[256,1024]{1,0:T(8,128)(2,1)S(1)}, u32[]{:S(2)}, u32[]{:S(2)}) %collective-permute-start.25) | collective-permute-done | bytes 524320 | tf_op jit(solution)/shard_map/ppermute | solution.py:473
  162.7 5.9 %feed_back_first.1 = (bf16[512,1024]{1,0:T(8,128)(2,1)S(1)}, bf16[256,1024]{1,0:T(8,128)(2,1)S(1)}, bf16[256,1024]{1,0:T(8,128)(2,1)S(1)}, f32[8,1024]{1,0:T(8,128)S(1)}) custom-call(bf16[256,1024]{1,0:T(8,128)(2,1)S(1)} %get-tuple-element.153.m0, bf16[256,1024]{1,0:T(8,128)(2,1)S(1)} %collective-permute-done.27.m2, ...), custom_call_target="tpu_custom_call" | custom-call | flops 53687092 | bytes 236748 | tf_op jit(solution)/shard_map/feed_back_first/pallas_call | solution.py:535
  168.6 12.2 %collective-permute-done.28.m1 = bf16[256,1024]{1,0:T(8,128)(2,1)S(1)} collective-permute-done((bf16[256,1024]{1,0:T(8,128)(2,1)S(1)}, bf16[256,1024]{1,0:T(8,128)(2,1)S(1)}, u32[]{:S(2)}, u32[]{:S(2)}) %collective-permute-start.28) | collective-permute-done | bytes 524320 | tf_op jit(solution)/shard_map/ppermute | solution.py:473
  182.7 5.9 %feed_back_second.1 = (bf16[512,1024]{1,0:T(8,128)(2,1)S(1)}, bf16[256,1024]{1,0:T(8,128)(2,1)S(1)}, bf16[512,1024]{1,0:T(8,128)(2,1)S(1)}, f32[8,1024]{1,0:T(8,128)S(1)}) custom-call(bf16[256,1024]{1,0:T(8,128)(2,1)S(1)} %collective-permute-done.28.m1, bf16[256,1024]{1,0:T(8,128)(2,1)S(1)} %collective-permute-done.29.m3, ...), custom_call_target="tpu_custom_call" | custom-call | flops 53687092 | bytes 263782 | tf_op jit(solution)/shard_map/feed_back_second/pallas_call | solution.py:535
  199.3 6.3 %collective-permute-done.31.x_in = bf16[256,1024]{1,0:T(8,128)(2,1)S(1)} collective-permute-done((bf16[256,1024]{1,0:T(8,128)(2,1)S(1)}, bf16[256,1024]{1,0:T(8,128)(2,1)S(1)}, u32[]{:S(2)}, u32[]{:S(2)}) %collective-permute-start.31) | collective-permute-done | bytes 524320 | tf_op jit(solution)/shard_map/ppermute | solution.py:473
  208.6 12.7 %collective-permute-done.33.come = bf16[4,128,1024]{2,1,0:T(8,128)(2,1)S(1)} collective-permute-done((bf16[4,128,1024]{2,1,0:T(8,128)(2,1)S(1)}, bf16[4,128,1024]{2,1,0:T(8,128)(2,1)S(1)}, u32[]{:S(2)}, u32[]{:S(2)}) %collective-permute-start.33) | collective-permute-done | bytes 1048608 | tf_op jit(solution)/shard_map/ppermute | solution.py:473
  223.4 6.0 %attend_back_first.1 = (bf16[1024,256]{1,0:T(8,128)(2,1)S(1)}, bf16[1024,384]{1,0:T(8,128)(2,1)S(1)}, f32[8,384]{1,0:T(8,128)S(1)}) custom-call(bf16[256,1024]{1,0:T(8,128)(2,1)S(1)} %get-tuple-element.177.a0, bf16[256,1024]{1,0:T(8,128)(2,1)S(1)} %collective-permute-done.32.a1, bf16[256,1024]{1,0:T(8,128)(2,1)S(1)} %collective-permute-done.34.a2, ...), custom_call_target="tpu_custom_call" | custom-call | flops 60397976 | bytes 190361 | tf_op jit(solution)/shard_map/attend_back_first/pallas_call | solution.py:535
  232.4 7.6 %attend_back_second.1 = (bf16[1024,384]{1,0:T(8,128)(2,1)S(1)}, f32[8,384]{1,0:T(8,128)S(1)}, bf16[256,1024]{1,0:T(8,128)(2,1)S(1)}, bf16[256,1024]{1,0:T(8,128)(2,1)S(1)}, bf16[512,1024]{1,0:T(8,128)(2,1)S(1)}) custom-call(bf16[1024,256]{1,0:T(8,128)(2,1)S(1)} %get-tuple-element.192.d_out, bf16[1024,384]{1,0:T(8,128)(2,1)S(1)} %get-tuple-element.189.grads.before, ...), custom_call_target="tpu_custom_call" | custom-call | flops 60397976 | bytes 236236 | tf_op jit(solution)/shard_map/attend_back_second/pallas_call | solution.py:535
  260.8 6.1 %collective-permute-done.57.come = bf16[2,128,1024]{2,1,0:T(8,128)(2,1)S(1)} collective-permute-done((bf16[2,128,1024]{2,1,0:T(8,128)(2,1)S(1)}, bf16[2,128,1024]{2,1,0:T(8,128)(2,1)S(1)}, u32[]{:S(2)}, u32[]{:S(2)}) %collective-permute-start.57) | collective-permute-done | bytes 524320 | tf_op jit(solution)/shard_map/ppermute | solution.py:483
  271.4 8.9 %collective-permute-done.58 = bf16[128,1024]{1,0:T(8,128)(2,1)S(1)} collective-permute-done((bf16[128,1024]{1,0:T(8,128)(2,1)S(1)}, bf16[128,1024]{1,0:T(8,128)(2,1)S(1)}, u32[]{:S(2)}, u32[]{:S(2)}) %collective-permute-start.58) | collective-permute-done | bytes 262176 | tf_op jit(solution)/shard_map/ppermute | solution.py:483
  283.5 7.3 %collective-permute-done.59.x_part = bf16[128,1024]{1,0:T(8,128)(2,1)S(1)} collective-permute-done((bf16[128,1024]{1,0:T(8,128)(2,1)S(1)}, bf16[128,1024]{1,0:T(8,128)(2,1)S(1)}, u32[]{:S(2)}, u32[]{:S(2)}) %collective-permute-start.59) | collective-permute-done | bytes 262176 | tf_op jit(solution)/shard_map/ppermute | solution.py:473
  292.1 10.0 %collective-permute-done.43 = bf16[128,640]{1,0:T(8,128)(2,1)S(1)} collective-permute-done((bf16[128,640]{1,0:T(8,128)(2,1)S(1)}, bf16[128,640]{1,0:T(8,128)(2,1)S(1)}, u32[]{:S(2)}, u32[]{:S(2)}) %collective-permute-start.43) | collective-permute-done | bytes 163872 | tf_op jit(solution)/shard_map/ppermute | solution.py:483
  302.1 4.2 %collective-permute-start.44 = (bf16[128,640]{1,0:T(8,128)(2,1)S(1)}, bf16[128,640]{1,0:T(8,128)(2,1)S(1)}, u32[]{:S(2)}, u32[]{:S(2)}) collective-permute-start(bf16[128,640]{1,0:T(8,128)(2,1)S(1)} %add_convert_fusion.6.own), channel_id=1, source_target_pairs={{0,8},{4,12},{8,0},{12,4},{16,24},{20,28},{24,16},{28,20},{1,9},{5... | collective-permute-start | bytes 491528 | tf_op jit(solution)/shard_map/ppermute | solution.py:473
  319.0 5.5 %collective-permute-done.51.y_part2 = bf16[2,136,384]{2,1,0:T(8,128)(2,1)S(1)} collective-permute-done((bf16[2,136,384]{2,1,0:T(8,128)(2,1)S(1)}, bf16[2,136,384]{2,1,0:T(8,128)(2,1)S(1)}, u32[]{:S(2)}, u32[]{:S(2)}) %collective-permute-start.51) | collective-permute-done | bytes 208928 | tf_op jit(solution)/shard_map/ppermute | solution.py:473
  (190 shorter events, 129.4 us)
Async XLA Ops:
  0.7 30.0 %collective-permute-start = (bf16[256,1024]{1,0:T(8,128)(2,1)}, bf16[256,1024]{1,0:T(8,128)(2,1)S(1)}, u32[]{:S(2)}, u32[]{:S(2)}) collective-permute-start(bf16[256,1024]{1,0:T(8,128)(2,1)} %param.18), channel_id=1, source_target_pairs={{0,0},{1,8},{2,4},{3,12},{4,10},{5,2},{6,14},{7,6},{8,1},{9,9},{10... | collective-permute-start | bytes 1572872 | tf_op jit(solution)/shard_map/ppermute | solution.py:1223
  14.0 16.7 %collective-permute-start.1 = (bf16[144,1024]{1,0:T(8,128)(2,1)S(1)}, bf16[144,1024]{1,0:T(8,128)(2,1)S(1)}, u32[]{:S(2)}, u32[]{:S(2)}) collective-permute-start(bf16[144,1024]{1,0:T(8,128)(2,1)S(1)} %dynamic-slice_bitcast_fusion), channel_id=1, source_target_pairs={{0,2},{1,3},{2,0},{3,1},{4,6},{5,7},{6,4},{7,5},{8,10},{9,11},{10,... | collective-permute-start | bytes 884744 | tf_op jit(solution)/shard_map/ppermute | solution.py:483
  30.7 21.2 %collective-permute-start.2 = (bf16[256,1024]{1,0:T(8,128)(2,1)S(1)}, bf16[256,1024]{1,0:T(8,128)(2,1)S(1)}, u32[]{:S(2)}, u32[]{:S(2)}) collective-permute-start(bf16[256,1024]{1,0:T(8,128)(2,1)S(1)} %collective-permute-done.x0.rows_in), channel_id=1, source_target_pairs={{0,8},{4,12},{8,0},{12,4},{16,24},{20,28},{24,16},{28,20},{1,9},{5... | collective-permute-start | bytes 1572872 | tf_op jit(solution)/shard_map/ppermute | solution.py:473
  55.6 20.9 %collective-permute-start.12 = (bf16[128,1024]{1,0:T(8,128)(2,1)S(1)}, bf16[128,1024]{1,0:T(8,128)(2,1)S(1)}, u32[]{:S(2)}, u32[]{:S(2)}) collective-permute-start(bf16[128,1024]{1,0:T(8,128)(2,1)S(1)} %dynamic-slice_bitcast_fusion.2), channel_id=1, source_target_pairs={{0,3},{1,2},{2,1},{3,0},{4,7},{5,6},{6,5},{7,4},{8,11},{9,10},{10,... | collective-permute-start | bytes 786440 | tf_op jit(solution)/shard_map/ppermute | solution.py:483
  79.4 36.7 %collective-permute-start.16 = (bf16[256,1024]{1,0:T(8,128)(2,1)S(1)}, bf16[256,1024]{1,0:T(8,128)(2,1)S(1)}, u32[]{:S(2)}, u32[]{:S(2)}) collective-permute-start(bf16[256,1024]{1,0:T(8,128)(2,1)S(1)} %copy-done.16), channel_id=1, source_target_pairs={{0,0},{1,8},{2,4},{3,12},{4,10},{5,2},{6,14},{7,6},{8,1},{9,9},{10... | collective-permute-start | bytes 1572872 | tf_op jit(solution)/shard_map/ppermute | solution.py:1250
  80.4 35.7 %collective-permute-start.15 = (bf16[3,128,1024]{2,1,0:T(8,128)(2,1)S(1)}, bf16[3,128,1024]{2,1,0:T(8,128)(2,1)S(1)}, u32[]{:S(2)}, u32[]{:S(2)}) collective-permute-start(bf16[3,128,1024]{2,1,0:T(8,128)(2,1)S(1)} %pad_maximum_fusion.2), channel_id=1, source_target_pairs={{0,16},{4,20},{8,24},{12,28},{16,0},{20,4},{24,8},{28,12},{1,17},{... | collective-permute-start | bytes 2359304 | tf_op jit(solution)/shard_map/ppermute | solution.py:473
  92.7 22.0 %collective-permute-start.19 = (bf16[128,1024]{1,0:T(8,128)(2,1)S(1)}, bf16[128,1024]{1,0:T(8,128)(2,1)S(1)}, u32[]{:S(2)}, u32[]{:S(2)}) collective-permute-start(bf16[128,1024]{1,0:T(8,128)(2,1)S(1)} %collective-permute-done.18.d2), channel_id=1, source_target_pairs={{0,1},{1,0},{2,3},{3,2},{4,5},{5,4},{6,7},{7,6},{8,9},{9,8},{10,11... | collective-permute-start | bytes 786440 | tf_op jit(solution)/shard_map/ppermute | solution.py:483
  92.9 23.2 %collective-permute-start.14 = (bf16[256,1024]{1,0:T(8,128)(2,1)S(1)}, bf16[256,1024]{1,0:T(8,128)(2,1)S(1)}, u32[]{:S(2)}, u32[]{:S(2)}) collective-permute-start(bf16[256,1024]{1,0:T(8,128)(2,1)S(1)} %add_convert_fusion.3), channel_id=1, source_target_pairs={{0,8},{4,12},{8,0},{12,4},{16,24},{20,28},{24,16},{28,20},{1,9},{5... | collective-permute-start | bytes 1572872 | tf_op jit(solution)/shard_map/ppermute | solution.py:473
  117.9 16.8 %collective-permute-start.22 = (bf16[256,1024]{1,0:T(8,128)(2,1)S(1)}, bf16[256,1024]{1,0:T(8,128)(2,1)S(1)}, u32[]{:S(2)}, u32[]{:S(2)}) collective-permute-start(bf16[256,1024]{1,0:T(8,128)(2,1)S(1)} %get-tuple-element.143.h0), channel_id=1, source_target_pairs={{0,8},{4,12},{8,0},{12,4},{16,24},{20,28},{24,16},{28,20},{1,9},{5... | collective-permute-start | bytes 1572872 | tf_op jit(solution)/shard_map/ppermute | solution.py:473
  160.8 20.0 %collective-permute-start.28 = (bf16[256,1024]{1,0:T(8,128)(2,1)S(1)}, bf16[256,1024]{1,0:T(8,128)(2,1)S(1)}, u32[]{:S(2)}, u32[]{:S(2)}) collective-permute-start(bf16[256,1024]{1,0:T(8,128)(2,1)S(1)} %get-tuple-element.153.m0), channel_id=1, source_target_pairs={{0,8},{4,12},{8,0},{12,4},{16,24},{20,28},{24,16},{28,20},{1,9},{5... | collective-permute-start | bytes 1572872 | tf_op jit(solution)/shard_map/ppermute | solution.py:473
  161.2 19.6 %collective-permute-start.26 = (bf16[256,1024]{1,0:T(8,128)(2,1)S(1)}, bf16[256,1024]{1,0:T(8,128)(2,1)S(1)}, u32[]{:S(2)}, u32[]{:S(2)}) collective-permute-start(bf16[256,1024]{1,0:T(8,128)(2,1)S(1)} %get-tuple-element.152), channel_id=1, source_target_pairs={{0,0},{8,1},{4,2},{12,3},{10,4},{2,5},{14,6},{6,7},{1,8},{9,9},{5,... | collective-permute-start | bytes 1572872 | tf_op jit(solution)/shard_map/ppermute | solution.py:1322
  195.1 26.1 %collective-permute-start.33 = (bf16[4,128,1024]{2,1,0:T(8,128)(2,1)S(1)}, bf16[4,128,1024]{2,1,0:T(8,128)(2,1)S(1)}, u32[]{:S(2)}, u32[]{:S(2)}) collective-permute-start(bf16[4,128,1024]{2,1,0:T(8,128)(2,1)S(1)} %get-tuple-element.169), channel_id=1, source_target_pairs={{0,16},{4,20},{8,24},{12,28},{16,0},{20,4},{24,8},{28,12},{1,17},{... | collective-permute-start | bytes 3145736 | tf_op jit(solution)/shard_map/ppermute | solution.py:473
  207.7 34.9 %collective-permute-start.36 = (bf16[4,128,1024]{2,1,0:T(8,128)(2,1)S(1)}, bf16[4,128,1024]{2,1,0:T(8,128)(2,1)S(1)}, u32[]{:S(2)}, u32[]{:S(2)}) collective-permute-start(bf16[4,128,1024]{2,1,0:T(8,128)(2,1)S(1)} %get-tuple-element.172), channel_id=1, source_target_pairs={{0,16},{4,20},{8,24},{12,28},{16,0},{20,4},{24,8},{28,12},{1,17},{... | collective-permute-start | bytes 3145736 | tf_op jit(solution)/shard_map/ppermute | solution.py:473
  221.5 21.1 %collective-permute-start.37 = (bf16[2,128,1024]{2,1,0:T(8,128)(2,1)S(1)}, bf16[2,128,1024]{2,1,0:T(8,128)(2,1)S(1)}, u32[]{:S(2)}, u32[]{:S(2)}) collective-permute-start(bf16[2,128,1024]{2,1,0:T(8,128)(2,1)S(1)} %get-tuple-element.179), channel_id=1, source_target_pairs={{0,1},{1,0},{2,3},{3,2},{4,5},{5,4},{6,7},{7,6},{8,9},{9,8},{10,11... | collective-permute-start | bytes 1572872 | tf_op jit(solution)/shard_map/ppermute | solution.py:483
  247.5 19.4 %collective-permute-start.57 = (bf16[2,128,1024]{2,1,0:T(8,128)(2,1)S(1)}, bf16[2,128,1024]{2,1,0:T(8,128)(2,1)S(1)}, u32[]{:S(2)}, u32[]{:S(2)}) collective-permute-start(bf16[2,128,1024]{2,1,0:T(8,128)(2,1)S(1)} %get-tuple-element.207), channel_id=1, source_target_pairs={{0,1},{1,0},{2,3},{3,2},{4,5},{5,4},{6,7},{7,6},{8,9},{9,8},{10,11... | collective-permute-start | bytes 1572872 | tf_op jit(solution)/shard_map/ppermute | solution.py:483
  247.6 21.1 %collective-permute-start.41 = (bf16[4,128,640]{2,1,0:T(8,128)(2,1)S(1)}, bf16[4,128,640]{2,1,0:T(8,128)(2,1)S(1)}, u32[]{:S(2)}, u32[]{:S(2)}) collective-permute-start(bf16[4,128,640]{2,1,0:T(8,128)(2,1)S(1)} %get-tuple-element.191), channel_id=1, source_target_pairs={{0,16},{4,20},{8,24},{12,28},{16,0},{20,4},{24,8},{28,12},{1,17},{... | collective-permute-start | bytes 1966088 | tf_op jit(solution)/shard_map/ppermute | solution.py:473
  248.6 18.6 %collective-permute-start.52 = (bf16[128,1024]{1,0:T(8,128)(2,1)S(1)}, bf16[128,1024]{1,0:T(8,128)(2,1)S(1)}, u32[]{:S(2)}, u32[]{:S(2)}) collective-permute-start(bf16[128,1024]{1,0:T(8,128)(2,1)S(1)} %get-tuple-element.224), channel_id=1, source_target_pairs={{0,2},{1,3},{2,0},{3,1},{4,6},{5,7},{6,4},{7,5},{8,10},{9,11},{10,... | collective-permute-start | bytes 786440 | tf_op jit(solution)/shard_map/ppermute | solution.py:483
  267.7 24.2 %collective-permute-start.47 = (bf16[4,136,384]{2,1,0:T(8,128)(2,1)S(1)}, bf16[4,136,384]{2,1,0:T(8,128)(2,1)S(1)}, u32[]{:S(2)}, u32[]{:S(2)}) collective-permute-start(bf16[4,136,384]{2,1,0:T(8,128)(2,1)S(1)} %get-tuple-element.205), channel_id=1, source_target_pairs={{0,16},{4,20},{8,24},{12,28},{16,0},{20,4},{24,8},{28,12},{1,17},{... | collective-permute-start | bytes 1253384 | tf_op jit(solution)/shard_map/ppermute | solution.py:473
  280.8 25.6 %collective-permute-start.40 = (bf16[256,1024]{1,0:T(8,128)(2,1)S(1)}, bf16[256,1024]{1,0:T(8,128)(2,1)S(1)}, u32[]{:S(2)}, u32[]{:S(2)}) collective-permute-start(bf16[256,1024]{1,0:T(8,128)(2,1)S(1)} %after_attention_back.1), channel_id=1, source_target_pairs={{0,0},{8,1},{4,2},{12,3},{10,4},{2,5},{14,6},{6,7},{1,8},{9,9},{5,... | collective-permute-start | bytes 1572872 | tf_op jit(solution)/shard_map/ppermute | solution.py:1404
  281.5 25.0 %collective-permute-start.54 = (bf16[2,128,1024]{2,1,0:T(8,128)(2,1)S(1)}, bf16[2,128,1024]{2,1,0:T(8,128)(2,1)S(1)}, u32[]{:S(2)}, u32[]{:S(2)}) collective-permute-start(bf16[2,128,1024]{2,1,0:T(8,128)(2,1)S(1)} %pad_maximum_fusion.7), channel_id=1, source_target_pairs={{0,16},{4,20},{8,24},{12,28},{16,0},{20,4},{24,8},{28,12},{1,17},{... | collective-permute-start | bytes 1572872 | tf_op jit(solution)/shard_map/ppermute | solution.py:473
  283.1 19.0 %collective-permute-start.43 = (bf16[128,640]{1,0:T(8,128)(2,1)S(1)}, bf16[128,640]{1,0:T(8,128)(2,1)S(1)}, u32[]{:S(2)}, u32[]{:S(2)}) collective-permute-start(bf16[128,640]{1,0:T(8,128)(2,1)S(1)} %get-tuple-element.214), channel_id=1, source_target_pairs={{0,2},{1,3},{2,0},{3,1},{4,6},{5,7},{6,4},{7,5},{8,10},{9,11},{10,... | collective-permute-start | bytes 491528 | tf_op jit(solution)/shard_map/ppermute | solution.py:483
  290.8 19.9 %collective-permute-start.60 = (bf16[2,128,1024]{2,1,0:T(8,128)(2,1)S(1)}, bf16[2,128,1024]{2,1,0:T(8,128)(2,1)S(1)}, u32[]{:S(2)}, u32[]{:S(2)}) collective-permute-start(bf16[2,128,1024]{2,1,0:T(8,128)(2,1)S(1)} %pad_maximum_fusion.8), channel_id=1, source_target_pairs={{0,16},{4,20},{8,24},{12,28},{16,0},{20,4},{24,8},{28,12},{1,17},{... | collective-permute-start | bytes 1572872 | tf_op jit(solution)/shard_map/ppermute | solution.py:473
  306.6 18.0 %collective-permute-start.55 = (bf16[4,128,1024]{2,1,0:T(8,128)(2,1)S(1)}, bf16[4,128,1024]{2,1,0:T(8,128)(2,1)S(1)}, u32[]{:S(2)}, u32[]{:S(2)}) collective-permute-start(bf16[4,128,1024]{2,1,0:T(8,128)(2,1)S(1)} %pad_maximum_fusion), channel_id=1, source_target_pairs={{0,4},{4,0},{8,12},{12,8},{16,20},{20,16},{24,28},{28,24},{1,5},{5... | collective-permute-start | bytes 3145736 | tf_op jit(solution)/shard_map/ppermute | solution.py:473
  310.8 17.2 %collective-permute-start.61 = (bf16[4,128,1024]{2,1,0:T(8,128)(2,1)S(1)}, bf16[4,128,1024]{2,1,0:T(8,128)(2,1)S(1)}, u32[]{:S(2)}, u32[]{:S(2)}) collective-permute-start(bf16[4,128,1024]{2,1,0:T(8,128)(2,1)S(1)} %pad_maximum_fusion.1), channel_id=1, source_target_pairs={{0,4},{4,0},{8,12},{12,8},{16,20},{20,16},{24,28},{28,24},{1,5},{5... | collective-permute-start | bytes 3145736 | tf_op jit(solution)/shard_map/ppermute | solution.py:473
  (55 other events, 446.1 us)
